TPU v7x, 256 devices: a whole 4x4x8 slice. The times are simulated.
256 devices in a mesh: seg: 4 (over y), tile: 64 (over z, x, core).
Axes of the slice: x: 4, y: 4, z: 8, core: 2. Of those that a mesh axis runs over, the one named last changes fastest.
Arguments:
- starting_warmth: float32 [2048, 65536], P('tile', 'seg'), may hold values from 0 to 1
- diffusivity_field: float32 [2048, 65536], P('tile', 'seg'), may hold values from 0.1 to 1
- emitter_mask: int32 [2048, 65536], P('tile', 'seg'), may hold values 0 or 1
Outputs:
- final_warmth: float32 [2048, 65536], P('tile', 'seg')
Inputs may be any that keep to these rules, and one draw needn't show every extreme that they name: `emitter_mask`: nonzero marks a source vertex.
All inputs are finite; a program needn't handle non-finite values. No bound on the sum of `emitter_mask` on one device may be relied on, other than what follows from the above.
Results may differ from a plain program's by a relative error of at most 0.00002.
Values sent between devices are 32-bit elements; how exact they have to be, the bound alone decides.
A program may use at most 128 MiB of HBM per device.

v0:
```python
import jax
import jax.numpy as jnp
from jax import lax
from jax.sharding import PartitionSpec as P

STEPS = 8


time_step = 0.24


def padded(shard, sides, width):
    for axis, dim in sides:
        size, length = (lax.axis_size(axis), shard.shape[dim])
        up = [(i, (i + 1) % size) for i in range(size - 1)]
        down = [(j, i) for i, j in up]
        last = lax.slice_in_dim(shard, length - width, length, axis=dim)
        first = lax.slice_in_dim(shard, 0, width, axis=dim)
        before = lax.ppermute(last, axis, up)
        after = lax.ppermute(first, axis, down)
        shard = jnp.concatenate([before, shard, after], axis=dim)
    return shard


def advance(bordered_grid, conduct, source, interior_region):
    height = bordered_grid.shape[0] - 2
    length = bordered_grid.shape[1] - 2
    middle_point = bordered_grid[1:-1, 1:-1]
    self_conductance = conduct[1:-1, 1:-1]
    flux_sum = jnp.zeros_like(middle_point)
    for row_off, col_off in ((0, 1), (2, 1), (1, 0), (1, 2)):
        adjacent_cell = bordered_grid[row_off : row_off + height, col_off : col_off + length]
        near_conduct = conduct[row_off : row_off + height, col_off : col_off + length]
        flux_sum = flux_sum + 0.5 * (self_conductance + near_conduct) * (
            adjacent_cell - middle_point
        )
    updated = middle_point + time_step * flux_sum
    updated = jnp.where(source, jnp.float32(1.0), updated)
    if interior_region is not None:
        updated = updated * interior_region
    return updated


def shards(starting_warmth, diffusivity_field, emitter_mask):
    rows_all, cols_all = starting_warmth.shape
    is_source = emitter_mask != 0
    present_warmth = starting_warmth
    stacked = jnp.stack([diffusivity_field, emitter_mask.astype(jnp.float32)])
    fixed_wide = padded(stacked, (("seg", 2), ("tile", 1)), 2)
    conduct_wide = fixed_wide[0]
    conduct_inner = conduct_wide[1:-1, 1:-1]
    source_margin = fixed_wide[1, 1:-1, 1:-1] > 0.5
    row_ids = lax.axis_index("tile") * rows_all + lax.iota(jnp.int32, rows_all + 2) - 1
    col_ids = lax.axis_index("seg") * cols_all + lax.iota(jnp.int32, cols_all + 2) - 1
    row_inside = (row_ids >= 0) & (row_ids < rows_all * lax.axis_size("tile"))
    column_interior = (col_ids >= 0) & (col_ids < cols_all * lax.axis_size("seg"))
    interior_region = (row_inside[:, None] & column_interior[None, :]).astype(jnp.float32)
    for pair_step in range(STEPS // 2):
        widened = padded(present_warmth, (("seg", 1), ("tile", 0)), 2)
        middle = advance(widened, conduct_wide, source_margin, interior_region)
        present_warmth = advance(middle, conduct_inner, is_source, None)
    return present_warmth


def solution(mesh):
    return jax.shard_map(
        shards,
        mesh=mesh,
        in_specs=(P("tile", "seg"), P("tile", "seg"), P("tile", "seg")),
        out_specs=P("tile", "seg"),
        check_vma=False,
    )
```

profile of v0, /device:TPU:111, one launch (start us, length us, event | category | flops | bytes accessed | tf_op | source)
XLA Modules:
  0.0 197.7 jit_solution(8490280880243570698)
XLA Ops:
  3.0 3.2 %collective-permute-start.4 = (f32[32,2]{1,0:T(8,128)S(1)}, f32[32,2]{1,0:T(8,128)S(1)}, u32[]{:S(2)}, u32[]{:S(2)}) collective-permute-start(f32[32,2]{1,0:T(8,128)S(1)} %get-tuple-element.36), channel_id=1, source_target_pairs={{0,64},{64,128},{128,192},{1,65},{65,129},{129,193},{2,66},{66,130... | collective-permute-start | bytes 776 | tf_op jit(solution)/shard_map/ppermute | solution.py:19
  10.1 3.2 %collective-permute-start = (f32[2,32,2]{2,1,0:T(8,128)S(1)}, f32[2,32,2]{2,1,0:T(8,128)S(1)}, u32[]{:S(2)}, u32[]{:S(2)}) collective-permute-start(f32[2,32,2]{2,1,0:T(8,128)S(1)} %get-tuple-element.20), channel_id=1, source_target_pairs={{0,64},{64,128},{128,192},{1,65},{65,129},{129,193},{2,66},{66,130... | collective-permute-start | bytes 1544 | tf_op jit(solution)/shard_map/ppermute | solution.py:19
  19.7 6.3 %collective-permute-start.6 = (f32[2,16388]{1,0:T(2,128)}, f32[2,16388]{1,0:T(2,128)S(1)}, u32[]{:S(2)}, u32[]{:S(2)}) collective-permute-start(f32[2,16388]{1,0:T(2,128)} %get-tuple-element.27), channel_id=1, source_target_pairs={{0,1},{1,2},{2,3},{3,4},{4,5},{5,6},{6,7},{7,8},{8,9},{9,10},{10,1... | collective-permute-start | bytes 393320 | tf_op jit(solution)/shard_map/ppermute | solution.py:19
  28.0 7.3 %concatenate.54 = f32[2,32,16388]{2,1,0:T(8,128)} concatenate(f32[2,32,2]{2,1,0:T(8,128)S(1)} %collective-permute-done, f32[2,32,16384]{2,1,0:T(8,128)} %pad_maximum_fusion, f32[2,32,2]{2,1,0:T(8,128)S(1)} %collective-permute-done.1), dimensions={2} | concatenate | bytes 8390656 | tf_op jit(solution)/shard_map/concatenate | solution.py:21
  37.1 7.2 %collective-permute-start.2 = (f32[2,2,16388]{2,1,0:T(2,128)S(1)}, f32[2,2,16388]{2,1,0:T(2,128)S(1)}, u32[]{:S(2)}, u32[]{:S(2)}) collective-permute-start(f32[2,2,16388]{2,1,0:T(2,128)S(1)} %get-tuple-element.17), channel_id=1, source_target_pairs={{0,1},{1,2},{2,3},{3,4},{4,5},{5,6},{6,7},{7,8},{8,9},{9,10},{10,1... | collective-permute-start | bytes 786632 | tf_op jit(solution)/shard_map/ppermute | solution.py:19
  47.6 7.7 %collective-permute-done.3 = f32[2,2,16388]{2,1,0:T(2,128)S(1)} collective-permute-done((f32[2,2,16388]{2,1,0:T(2,128)S(1)}, f32[2,2,16388]{2,1,0:T(2,128)S(1)}, u32[]{:S(2)}, u32[]{:S(2)}) %collective-permute-start.3) | collective-permute-done | bytes 262240 | tf_op jit(solution)/shard_map/ppermute | solution.py:20
  58.4 10.8 %and_select_fusion.3 = (f32[34,16386]{1,0:T(8,128)S(1)}, f32[34,16386]{1,0:T(8,128)S(1)}, f32[34,16386]{1,0:T(8,128)}, f32[34,16386]{1,0:T(8,128)}, f32[34,16386]{1,0:T(8,128)}, /*index=5*/pred[34,16386]{1,0:T(8,128)(4,1)S(1)}) fusion(f32[36,16388]{1,0:T(8,128)S(1)} %pad_maximum_fusion.10, f32[2,16388]{1,0:T(2,128)} %copy-done.16, f32[32,16388]{1,0:T(8,128)} %copy-done.7, ...), kind=kLoop, calls=%fused_computation.9 | loop fusion | flops 15042348 | bytes 34132360 | tf_op jit(solution)/shard_map/mul | solution.py:40
  69.3 8.3 %fusion.87 = (f32[32,16384]{1,0:T(8,128)S(1)}, f32[32,16384]{1,0:T(8,128)}, f32[32,16384]{1,0:T(8,128)}, f32[32,16384]{1,0:T(8,128)}, f32[32,16384]{1,0:T(8,128)}, /*index=5*/pred[32,16384]{1,0:T(8,128)(4,1)}) fusion(f32[34,16386]{1,0:T(8,128)S(1)} %get-tuple-element.11, f32[36,16388]{1,0:T(8,128)S(1)} %slice_bitcast_fusion, s32[32,16384]{1,0:T(8,128)} %param.5), kind=kLoop, calls=%fused_computation.136 | loop fusion | flops 12058624 | bytes 34078720 | tf_op jit(solution)/shard_map/jit(_where)/select_n | solution.py:38
  81.1 3.2 %collective-permute-start.8 = (f32[32,2]{1,0:T(8,128)S(1)}, f32[32,2]{1,0:T(8,128)S(1)}, u32[]{:S(2)}, u32[]{:S(2)}) collective-permute-start(f32[32,2]{1,0:T(8,128)S(1)} %get-tuple-element.34), channel_id=1, source_target_pairs={{0,64},{64,128},{128,192},{1,65},{65,129},{129,193},{2,66},{66,130... | collective-permute-start | bytes 776 | tf_op jit(solution)/shard_map/ppermute | solution.py:19
  85.6 4.2 %concatenate.60 = f32[32,16388]{1,0:T(8,128)} concatenate(f32[32,2]{1,0:T(8,128)S(1)} %collective-permute-done.8, f32[32,16384]{1,0:T(8,128)} %copy-done.9, f32[32,2]{1,0:T(8,128)S(1)} %collective-permute-done.9), dimensions={1} | concatenate | bytes 4195328 | tf_op jit(solution)/shard_map/concatenate | solution.py:21
  91.2 3.3 %collective-permute-start.10 = (f32[2,16388]{1,0:T(2,128)S(1)}, f32[2,16388]{1,0:T(2,128)S(1)}, u32[]{:S(2)}, u32[]{:S(2)}) collective-permute-start(f32[2,16388]{1,0:T(2,128)S(1)} %get-tuple-element.25), channel_id=1, source_target_pairs={{0,1},{1,2},{2,3},{3,4},{4,5},{5,6},{6,7},{7,8},{8,9},{9,10},{10,1... | collective-permute-start | bytes 393320 | tf_op jit(solution)/shard_map/ppermute | solution.py:19
  96.6 7.5 %collective-permute-done.11 = f32[2,16388]{1,0:T(2,128)S(1)} collective-permute-done((f32[2,16388]{1,0:T(2,128)S(1)}, f32[2,16388]{1,0:T(2,128)S(1)}, u32[]{:S(2)}, u32[]{:S(2)}) %collective-permute-start.11) | collective-permute-done | bytes 131136 | tf_op jit(solution)/shard_map/ppermute | solution.py:20
  106.1 5.5 %and_select_fusion.2 = f32[34,16386]{1,0:T(8,128)S(1)} fusion(pred[34,16386]{1,0:T(8,128)(4,1)S(1)} %get-tuple-element.16, f32[34,16386]{1,0:T(8,128)} %get-tuple-element.15, f32[36,16388]{1,0:T(8,128)S(1)} %pad_maximum_fusion.11, f32[34,16386]{1,0:T(8,128)S(1)} %copy-done.3, f32[34,16386]{1,0:T(8,128)S(1)} %copy-done, ...), kind=kLoop, calls=%fused_computation.8 | loop fusion | flops 10028232 | bytes 20761384 | tf_op jit(solution)/shard_map/mul | solution.py:40
  111.6 5.8 %fusion.77 = f32[32,16384]{1,0:T(8,128)S(1)} fusion(pred[32,16384]{1,0:T(8,128)(4,1)S(1)} %copy-done.13, f32[32,16384]{1,0:T(8,128)} %get-tuple-element.9, f32[34,16386]{1,0:T(8,128)S(1)} %and_select_fusion.2, f32[32,16384]{1,0:T(8,128)} %get-tuple-element.8, f32[32,16384]{1,0:T(8,128)} %get-tuple-element.7, f32[32,16384]{1,0:T(8,128)} %get-tuple-element.6), kind=kLoop, calls=%fused_computation.122 | loop fusion | flops 7340032 | bytes 21495808 | tf_op jit(solution)/shard_map/jit(_where)/select_n | solution.py:38
  120.8 3.4 %collective-permute-start.12 = (f32[32,2]{1,0:T(8,128)S(1)}, f32[32,2]{1,0:T(8,128)S(1)}, u32[]{:S(2)}, u32[]{:S(2)}) collective-permute-start(f32[32,2]{1,0:T(8,128)S(1)} %get-tuple-element.32), channel_id=1, source_target_pairs={{0,64},{64,128},{128,192},{1,65},{65,129},{129,193},{2,66},{66,130... | collective-permute-start | bytes 776 | tf_op jit(solution)/shard_map/ppermute | solution.py:19
  125.3 4.2 %concatenate.64 = f32[32,16388]{1,0:T(8,128)} concatenate(f32[32,2]{1,0:T(8,128)S(1)} %collective-permute-done.12, f32[32,16384]{1,0:T(8,128)} %copy-done.10, f32[32,2]{1,0:T(8,128)S(1)} %collective-permute-done.13), dimensions={1} | concatenate | bytes 4195328 | tf_op jit(solution)/shard_map/concatenate | solution.py:21
  135.9 7.7 %collective-permute-done.15 = f32[2,16388]{1,0:T(2,128)S(1)} collective-permute-done((f32[2,16388]{1,0:T(2,128)S(1)}, f32[2,16388]{1,0:T(2,128)S(1)}, u32[]{:S(2)}, u32[]{:S(2)}) %collective-permute-start.15) | collective-permute-done | bytes 131136 | tf_op jit(solution)/shard_map/ppermute | solution.py:20
  145.5 5.5 %and_select_fusion.1 = f32[34,16386]{1,0:T(8,128)S(1)} fusion(pred[34,16386]{1,0:T(8,128)(4,1)S(1)} %get-tuple-element.16, f32[34,16386]{1,0:T(8,128)} %get-tuple-element.15, f32[36,16388]{1,0:T(8,128)S(1)} %pad_maximum_fusion.12, f32[34,16386]{1,0:T(8,128)S(1)} %copy-done.4, f32[34,16386]{1,0:T(8,128)S(1)} %copy-done.1, ...), kind=kLoop, calls=%fused_computation.7 | loop fusion | flops 10028232 | bytes 20761384 | tf_op jit(solution)/shard_map/mul | solution.py:40
  151.1 5.8 %fusion.67 = f32[32,16384]{1,0:T(8,128)S(1)} fusion(pred[32,16384]{1,0:T(8,128)(4,1)S(1)} %copy-done.14, f32[32,16384]{1,0:T(8,128)} %get-tuple-element.9, f32[34,16386]{1,0:T(8,128)S(1)} %and_select_fusion.1, f32[32,16384]{1,0:T(8,128)} %get-tuple-element.8, f32[32,16384]{1,0:T(8,128)} %get-tuple-element.7, f32[32,16384]{1,0:T(8,128)} %get-tuple-element.6), kind=kLoop, calls=%fused_computation.108 | loop fusion | flops 7340032 | bytes 21495808 | tf_op jit(solution)/shard_map/jit(_where)/select_n | solution.py:38
  160.2 3.6 %collective-permute-start.16 = (f32[32,2]{1,0:T(8,128)S(1)}, f32[32,2]{1,0:T(8,128)S(1)}, u32[]{:S(2)}, u32[]{:S(2)}) collective-permute-start(f32[32,2]{1,0:T(8,128)S(1)} %get-tuple-element.30), channel_id=1, source_target_pairs={{0,64},{64,128},{128,192},{1,65},{65,129},{129,193},{2,66},{66,130... | collective-permute-start | bytes 776 | tf_op jit(solution)/shard_map/ppermute | solution.py:19
  164.7 4.2 %concatenate.68 = f32[32,16388]{1,0:T(8,128)} concatenate(f32[32,2]{1,0:T(8,128)S(1)} %collective-permute-done.16, f32[32,16384]{1,0:T(8,128)} %copy-done.11, f32[32,2]{1,0:T(8,128)S(1)} %collective-permute-done.17), dimensions={1} | concatenate | bytes 4195328 | tf_op jit(solution)/shard_map/concatenate | solution.py:21
  175.6 7.5 %collective-permute-done.19 = f32[2,16388]{1,0:T(2,128)S(1)} collective-permute-done((f32[2,16388]{1,0:T(2,128)S(1)}, f32[2,16388]{1,0:T(2,128)S(1)}, u32[]{:S(2)}, u32[]{:S(2)}) %collective-permute-start.19) | collective-permute-done | bytes 131136 | tf_op jit(solution)/shard_map/ppermute | solution.py:20
  185.0 5.5 %and_select_fusion = f32[34,16386]{1,0:T(8,128)S(1)} fusion(pred[34,16386]{1,0:T(8,128)(4,1)S(1)} %get-tuple-element.16, f32[34,16386]{1,0:T(8,128)} %get-tuple-element.15, f32[36,16388]{1,0:T(8,128)S(1)} %pad_maximum_fusion.13, f32[34,16386]{1,0:T(8,128)S(1)} %copy-done.5, f32[34,16386]{1,0:T(8,128)S(1)} %copy-done.2, ...), kind=kLoop, calls=%fused_computation.6 | loop fusion | flops 10028232 | bytes 20761384 | tf_op jit(solution)/shard_map/mul | solution.py:40
  190.5 7.2 %fusion.57 = f32[32,16384]{1,0:T(8,128)} fusion(pred[32,16384]{1,0:T(8,128)(4,1)S(1)} %copy-done.15, f32[32,16384]{1,0:T(8,128)} %get-tuple-element.9, f32[34,16386]{1,0:T(8,128)S(1)} %and_select_fusion, f32[32,16384]{1,0:T(8,128)} %get-tuple-element.8, f32[32,16384]{1,0:T(8,128)} %get-tuple-element.7, f32[32,16384]{1,0:T(8,128)} %get-tuple-element.6), kind=kLoop, calls=%fused_computation.94 | loop fusion | flops 7340032 | bytes 21495808 | tf_op jit(solution)/shard_map/jit(_where)/select_n | solution.py:38
  (83 shorter events, 58.9 us)
Async XLA Ops:
  1.0 14.7 %collective-permute-start.5 = (f32[32,2]{1,0:T(8,128)S(1)}, f32[32,2]{1,0:T(8,128)S(1)}, u32[]{:S(2)}, u32[]{:S(2)}) collective-permute-start(f32[32,2]{1,0:T(8,128)S(1)} %get-tuple-element.35), channel_id=1, source_target_pairs={{64,0},{128,64},{192,128},{65,1},{129,65},{193,129},{66,2},{130,66... | collective-permute-start | bytes 776 | tf_op jit(solution)/shard_map/ppermute | solution.py:20
  3.0 12.6 %collective-permute-start.4 = (f32[32,2]{1,0:T(8,128)S(1)}, f32[32,2]{1,0:T(8,128)S(1)}, u32[]{:S(2)}, u32[]{:S(2)}) collective-permute-start(f32[32,2]{1,0:T(8,128)S(1)} %get-tuple-element.36), channel_id=1, source_target_pairs={{0,64},{64,128},{128,192},{1,65},{65,129},{129,193},{2,66},{66,130... | collective-permute-start | bytes 776 | tf_op jit(solution)/shard_map/ppermute | solution.py:19
  8.1 19.9 %collective-permute-start.1 = (f32[2,32,2]{2,1,0:T(8,128)S(1)}, f32[2,32,2]{2,1,0:T(8,128)S(1)}, u32[]{:S(2)}, u32[]{:S(2)}) collective-permute-start(f32[2,32,2]{2,1,0:T(8,128)S(1)} %get-tuple-element.19), channel_id=1, source_target_pairs={{64,0},{128,64},{192,128},{65,1},{129,65},{193,129},{66,2},{130,66... | collective-permute-start | bytes 1544 | tf_op jit(solution)/shard_map/ppermute | solution.py:20
  10.1 17.8 %collective-permute-start = (f32[2,32,2]{2,1,0:T(8,128)S(1)}, f32[2,32,2]{2,1,0:T(8,128)S(1)}, u32[]{:S(2)}, u32[]{:S(2)}) collective-permute-start(f32[2,32,2]{2,1,0:T(8,128)S(1)} %get-tuple-element.20), channel_id=1, source_target_pairs={{0,64},{64,128},{128,192},{1,65},{65,129},{129,193},{2,66},{66,130... | collective-permute-start | bytes 1544 | tf_op jit(solution)/shard_map/ppermute | solution.py:19
  18.8 27.5 %copy-start.7 = (f32[32,16388]{1,0:T(8,128)}, f32[32,16388]{1,0:T(8,128)S(1)}, u32[]{:S(2)}) copy-start(f32[32,16388]{1,0:T(8,128)S(1)} %concatenate.56) | copy-start | bytes 6292996
  19.7 26.5 %collective-permute-start.6 = (f32[2,16388]{1,0:T(2,128)}, f32[2,16388]{1,0:T(2,128)S(1)}, u32[]{:S(2)}, u32[]{:S(2)}) collective-permute-start(f32[2,16388]{1,0:T(2,128)} %get-tuple-element.27), channel_id=1, source_target_pairs={{0,1},{1,2},{2,3},{3,4},{4,5},{5,6},{6,7},{7,8},{8,9},{9,10},{10,1... | collective-permute-start | bytes 393320 | tf_op jit(solution)/shard_map/ppermute | solution.py:19
  26.0 20.2 %collective-permute-start.7 = (f32[2,16388]{1,0:T(2,128)S(1)}, f32[2,16388]{1,0:T(2,128)S(1)}, u32[]{:S(2)}, u32[]{:S(2)}) collective-permute-start(f32[2,16388]{1,0:T(2,128)S(1)} %get-tuple-element.28), channel_id=1, source_target_pairs={{1,0},{2,1},{3,2},{4,3},{5,4},{6,5},{7,6},{8,7},{9,8},{10,9},{11,1... | collective-permute-start | bytes 393320 | tf_op jit(solution)/shard_map/ppermute | solution.py:20
  37.1 18.3 %copy-start.8 = (f32[2,32,16388]{2,1,0:T(8,128)S(1)}, f32[2,32,16388]{2,1,0:T(8,128)}, u32[]{:S(2)}) copy-start(f32[2,32,16388]{2,1,0:T(8,128)} %concatenate.54) | copy-start | bytes 12585988
  37.1 10.6 %collective-permute-start.2 = (f32[2,2,16388]{2,1,0:T(2,128)S(1)}, f32[2,2,16388]{2,1,0:T(2,128)S(1)}, u32[]{:S(2)}, u32[]{:S(2)}) collective-permute-start(f32[2,2,16388]{2,1,0:T(2,128)S(1)} %get-tuple-element.17), channel_id=1, source_target_pairs={{0,1},{1,2},{2,3},{3,4},{4,5},{5,6},{6,7},{7,8},{8,9},{9,10},{10,1... | collective-permute-start | bytes 786632 | tf_op jit(solution)/shard_map/ppermute | solution.py:19
  44.3 11.0 %collective-permute-start.3 = (f32[2,2,16388]{2,1,0:T(2,128)S(1)}, f32[2,2,16388]{2,1,0:T(2,128)S(1)}, u32[]{:S(2)}, u32[]{:S(2)}) collective-permute-start(f32[2,2,16388]{2,1,0:T(2,128)S(1)} %get-tuple-element.18), channel_id=1, source_target_pairs={{1,0},{2,1},{3,2},{4,3},{5,4},{6,5},{7,6},{8,7},{9,8},{10,9},{11,1... | collective-permute-start | bytes 786632 | tf_op jit(solution)/shard_map/ppermute | solution.py:20
  79.0 5.3 %collective-permute-start.9 = (f32[32,2]{1,0:T(8,128)S(1)}, f32[32,2]{1,0:T(8,128)S(1)}, u32[]{:S(2)}, u32[]{:S(2)}) collective-permute-start(f32[32,2]{1,0:T(8,128)S(1)} %get-tuple-element.33), channel_id=1, source_target_pairs={{64,0},{128,64},{192,128},{65,1},{129,65},{193,129},{66,2},{130,66... | collective-permute-start | bytes 776 | tf_op jit(solution)/shard_map/ppermute | solution.py:20
  81.1 4.5 %collective-permute-start.8 = (f32[32,2]{1,0:T(8,128)S(1)}, f32[32,2]{1,0:T(8,128)S(1)}, u32[]{:S(2)}, u32[]{:S(2)}) collective-permute-start(f32[32,2]{1,0:T(8,128)S(1)} %get-tuple-element.34), channel_id=1, source_target_pairs={{0,64},{64,128},{128,192},{1,65},{65,129},{129,193},{2,66},{66,130... | collective-permute-start | bytes 776 | tf_op jit(solution)/shard_map/ppermute | solution.py:19
  89.7 16.3 %copy-start.3 = (f32[34,16386]{1,0:T(8,128)S(1)}, f32[34,16386]{1,0:T(8,128)}, u32[]{:S(2)}) copy-start(f32[34,16386]{1,0:T(8,128)} %get-tuple-element.14) | copy-start | bytes 6685492
  91.2 5.4 %collective-permute-start.10 = (f32[2,16388]{1,0:T(2,128)S(1)}, f32[2,16388]{1,0:T(2,128)S(1)}, u32[]{:S(2)}, u32[]{:S(2)}) collective-permute-start(f32[2,16388]{1,0:T(2,128)S(1)} %get-tuple-element.25), channel_id=1, source_target_pairs={{0,1},{1,2},{2,3},{3,4},{4,5},{5,6},{6,7},{7,8},{8,9},{9,10},{10,1... | collective-permute-start | bytes 393320 | tf_op jit(solution)/shard_map/ppermute | solution.py:19
  94.5 9.6 %collective-permute-start.11 = (f32[2,16388]{1,0:T(2,128)S(1)}, f32[2,16388]{1,0:T(2,128)S(1)}, u32[]{:S(2)}, u32[]{:S(2)}) collective-permute-start(f32[2,16388]{1,0:T(2,128)S(1)} %get-tuple-element.26), channel_id=1, source_target_pairs={{1,0},{2,1},{3,2},{4,3},{5,4},{6,5},{7,6},{8,7},{9,8},{10,9},{11,1... | collective-permute-start | bytes 393320 | tf_op jit(solution)/shard_map/ppermute | solution.py:20
  118.9 5.3 %collective-permute-start.13 = (f32[32,2]{1,0:T(8,128)S(1)}, f32[32,2]{1,0:T(8,128)S(1)}, u32[]{:S(2)}, u32[]{:S(2)}) collective-permute-start(f32[32,2]{1,0:T(8,128)S(1)} %get-tuple-element.31), channel_id=1, source_target_pairs={{64,0},{128,64},{192,128},{65,1},{129,65},{193,129},{66,2},{130,66... | collective-permute-start | bytes 776 | tf_op jit(solution)/shard_map/ppermute | solution.py:20
  120.8 4.5 %collective-permute-start.12 = (f32[32,2]{1,0:T(8,128)S(1)}, f32[32,2]{1,0:T(8,128)S(1)}, u32[]{:S(2)}, u32[]{:S(2)}) collective-permute-start(f32[32,2]{1,0:T(8,128)S(1)} %get-tuple-element.32), channel_id=1, source_target_pairs={{0,64},{64,128},{128,192},{1,65},{65,129},{129,193},{2,66},{66,130... | collective-permute-start | bytes 776 | tf_op jit(solution)/shard_map/ppermute | solution.py:19
  129.4 16.1 %copy-start.4 = (f32[34,16386]{1,0:T(8,128)S(1)}, f32[34,16386]{1,0:T(8,128)}, u32[]{:S(2)}) copy-start(f32[34,16386]{1,0:T(8,128)} %get-tuple-element.14) | copy-start | bytes 6685492
  130.9 5.0 %collective-permute-start.14 = (f32[2,16388]{1,0:T(2,128)S(1)}, f32[2,16388]{1,0:T(2,128)S(1)}, u32[]{:S(2)}, u32[]{:S(2)}) collective-permute-start(f32[2,16388]{1,0:T(2,128)S(1)} %get-tuple-element.23), channel_id=1, source_target_pairs={{0,1},{1,2},{2,3},{3,4},{4,5},{5,6},{6,7},{7,8},{8,9},{9,10},{10,1... | collective-permute-start | bytes 393320 | tf_op jit(solution)/shard_map/ppermute | solution.py:19
  134.0 9.6 %collective-permute-start.15 = (f32[2,16388]{1,0:T(2,128)S(1)}, f32[2,16388]{1,0:T(2,128)S(1)}, u32[]{:S(2)}, u32[]{:S(2)}) collective-permute-start(f32[2,16388]{1,0:T(2,128)S(1)} %get-tuple-element.24), channel_id=1, source_target_pairs={{1,0},{2,1},{3,2},{4,3},{5,4},{6,5},{7,6},{8,7},{9,8},{10,9},{11,1... | collective-permute-start | bytes 393320 | tf_op jit(solution)/shard_map/ppermute | solution.py:20
  158.3 5.6 %collective-permute-start.17 = (f32[32,2]{1,0:T(8,128)S(1)}, f32[32,2]{1,0:T(8,128)S(1)}, u32[]{:S(2)}, u32[]{:S(2)}) collective-permute-start(f32[32,2]{1,0:T(8,128)S(1)} %get-tuple-element.29), channel_id=1, source_target_pairs={{64,0},{128,64},{192,128},{65,1},{129,65},{193,129},{66,2},{130,66... | collective-permute-start | bytes 776 | tf_op jit(solution)/shard_map/ppermute | solution.py:20
  160.2 4.5 %collective-permute-start.16 = (f32[32,2]{1,0:T(8,128)S(1)}, f32[32,2]{1,0:T(8,128)S(1)}, u32[]{:S(2)}, u32[]{:S(2)}) collective-permute-start(f32[32,2]{1,0:T(8,128)S(1)} %get-tuple-element.30), channel_id=1, source_target_pairs={{0,64},{64,128},{128,192},{1,65},{65,129},{129,193},{2,66},{66,130... | collective-permute-start | bytes 776 | tf_op jit(solution)/shard_map/ppermute | solution.py:19
  170.3 5.2 %collective-permute-start.18 = (f32[2,16388]{1,0:T(2,128)S(1)}, f32[2,16388]{1,0:T(2,128)S(1)}, u32[]{:S(2)}, u32[]{:S(2)}) collective-permute-start(f32[2,16388]{1,0:T(2,128)S(1)} %get-tuple-element.21), channel_id=1, source_target_pairs={{0,1},{1,2},{2,3},{3,4},{4,5},{5,6},{6,7},{7,8},{8,9},{9,10},{10,1... | collective-permute-start | bytes 393320 | tf_op jit(solution)/shard_map/ppermute | solution.py:19
  173.4 9.6 %collective-permute-start.19 = (f32[2,16388]{1,0:T(2,128)S(1)}, f32[2,16388]{1,0:T(2,128)S(1)}, u32[]{:S(2)}, u32[]{:S(2)}) collective-permute-start(f32[2,16388]{1,0:T(2,128)S(1)} %get-tuple-element.22), channel_id=1, source_target_pairs={{1,0},{2,1},{3,2},{4,3},{5,4},{6,5},{7,6},{8,7},{9,8},{10,9},{11,1... | collective-permute-start | bytes 393320 | tf_op jit(solution)/shard_map/ppermute | solution.py:20
  (13 other events, 100.8 us)
where the time goes:
time: 200 us; the launch traced here: 198 us
  other arithmetic  65.3 us (33%)
  starting transfers between devices  59.6 us (30%)
  local copies, waits for them, and re-layouts  37.6 us (19%)
  waiting for transfers between devices  34.6 us (17%)
    ppermute x10, starting transfers between devices, padded(): before = lax.ppermute(last, axis, up)  39.6 us
    ppermute x10, waiting for transfers between devices, padded(): after = lax.ppermute(first, axis, down)  30.4 us
    mul x4, other arithmetic, advance(): updated = updated * interior_region  27.4 us
    select_n x4, other arithmetic, advance(): updated = jnp.where(source, jnp.float32(1.0), updated)  27.2 us
    concatenate x5, local copies, waits for them, and re-layouts, padded(): shard = jnp.concatenate([before, shard, after], axis=dim)  22.9 us
    ppermute x10, starting transfers between devices, padded(): after = lax.ppermute(first, axis, down)  20 us
    slice x5, local copies, waits for them, and re-layouts, padded(): last = lax.slice_in_dim(shard, length - width, length, axis=dim)  6.99 us
    concatenate x5, other arithmetic, padded(): shard = jnp.concatenate([before, shard, after], axis=dim)  6.63 us
  transfers between devices with their start and end apart: 20, of which 8 were waited for; matrix products, arithmetic and copies ran while one was open for 9% of the time, Pallas kernels for 0%

commit v1 on v0

v1 whole, which is shorter than its diff:
```python
import functools

import jax
import jax.numpy as jnp
from jax import lax
from jax.experimental import pallas as pl
from jax.experimental.pallas import tpu as pltpu
from jax.sharding import PartitionSpec as P

STEPS = 8
FACE = 0.24 * 0.5
ROWS = 32
GHOST = 4
NV = 16
MESH = pl.DeviceIdType.MESH

LINES = ((1, 1), (2, 1), (2, 2), (3, 2), (3, 3), (4, 3), (4, 4))


def at(row):
    return row + GHOST


def shift_east(row, lane):
    turned = [pltpu.roll(x, 127, 1) for x in row]
    turned.append(pltpu.roll(turned[0], 7, 0))
    return [jnp.where(lane == 127, turned[v + 1], turned[v]) for v in range(NV)]


def shift_west(row, lane):
    turned = [pltpu.roll(x, 1, 1) for x in row]
    before = [pltpu.roll(turned[-1], 1, 0)] + turned[:-1]
    return [jnp.where(lane == 0, before[v], turned[v]) for v in range(NV)]


def load(ref, row):
    return [ref[v, row] for v in range(NV)]


def kernel(
    f_in, c_in, m_in, out,
    heat, cond, mask, east, south, keep,
    edge_fc, edge_m, edge_out,
    load_sem, edge_load_sem, send_sem, recv_sem, side_send, side_recv, out_sem,
):
    tile = lax.axis_index("tile")
    seg = lax.axis_index("seg")
    n_tile = lax.axis_size("tile")
    n_seg = lax.axis_size("seg")
    has_up = tile > 0
    has_down = tile < n_tile - 1
    has_west = seg > 0
    has_east = seg < n_seg - 1
    lane = lax.broadcasted_iota(jnp.int32, (8, 128), 1)

    def edge_loads():
        copies = []
        for piece, (s, v) in enumerate(((0, 0), (7, 15))):
            for k, src in enumerate((f_in, c_in)):
                copies.append(pltpu.make_async_copy(
                    src.at[:, s, v], edge_fc.at[piece, k, pl.ds(1, 4)],
                    edge_load_sem.at[3 * piece + k]))
            copies.append(pltpu.make_async_copy(
                m_in.at[:, s, v], edge_m.at[piece, pl.ds(1, 4)],
                edge_load_sem.at[3 * piece + 2]))
        return copies

    arrays = ((f_in, heat.at[0]), (c_in, cond), (m_in, mask))

    def block_load(k, block):
        src, dst = arrays[k]
        for s in range(8):
            pltpu.make_async_copy(
                src.at[block, s], dst.at[:, pl.ds(at(8 * block), 8), s, :],
                load_sem.at[k, block]).start()

    def block_wait(k, block):
        dst = arrays[k][1].at[:, pl.ds(at(8 * block), 8)]
        pltpu.make_async_copy(dst, dst, load_sem.at[k, block]).wait()

    for block in (0, 3):
        for k in (0, 1):
            block_load(k, block)
    for copy in edge_loads():
        copy.start()
    for block in (0, 3):
        block_load(2, block)
    for block in (1, 2):
        for k in (1, 0, 2):
            block_load(k, block)

    barrier = pltpu.get_barrier_semaphore()
    sides = (
        (has_up, {"tile": tile - 1}), (has_down, {"tile": tile + 1}),
        (has_west, {"seg": seg - 1}), (has_east, {"seg": seg + 1}),
    )
    for there, device in sides:
        @pl.when(there)
        def _():
            pl.semaphore_signal(barrier, inc=1, device_id=device, device_id_type=MESH)
    count = sum(there.astype(jnp.int32) for there, _ in sides)
    pl.semaphore_wait(barrier, count)

    def rows_of(direction, near, far):
        if direction == 0:
            return near - 1, ROWS + near - 1, far - near + 1
        return ROWS - far, -far, far - near + 1

    def remote(direction, slot, src, dst):
        device = {"tile": tile - 1 if direction == 0 else tile + 1}
        return pltpu.make_async_remote_copy(
            src_ref=src, dst_ref=dst,
            send_sem=send_sem.at[direction, slot], recv_sem=recv_sem.at[direction, slot],
            device_id=device, device_id_type=MESH)

    def tile_copy(direction, slot):
        if slot == 0:
            ref, near, far = heat.at[0], 1, 1
        elif slot == 1:
            ref, near, far = cond, 1, 1
        elif slot == 2:
            ref, near, far = cond, 2, 4
        elif slot == 3:
            ref, near, far = mask, 1, 3
        elif slot < 6:
            block = 1 if direction == 0 else 4
            land = 5 if direction == 0 else 0
            if slot == 4:
                return remote(direction, slot, edge_fc.at[:, :, block], edge_fc.at[:, :, land])
            return remote(direction, slot, edge_m.at[:, block], edge_m.at[:, land])
        else:
            distance, time = LINES[slot - 6]
            ref, near, far = heat.at[time % 2], distance, distance
        src, dst, count = rows_of(direction, near, far)
        return remote(direction, slot, ref.at[:, pl.ds(at(src), count)],
                      ref.at[:, pl.ds(at(dst), count)])

    def send(slot):
        for direction, there in ((0, has_up), (1, has_down)):
            @pl.when(there)
            def _():
                tile_copy(direction, slot).start()

    def sent(slot):
        for direction, there in ((0, has_up), (1, has_down)):
            @pl.when(there)
            def _():
                tile_copy(direction, slot).wait_send()

    def received(slot):
        for direction, there in ((0, has_down), (1, has_up)):
            @pl.when(there)
            def _():
                tile_copy(direction, slot).wait_recv()

    def side_copy(direction, kind):
        device = {"seg": seg - 1 if direction == 0 else seg + 1}
        ref = edge_m if kind else edge_fc
        if kind:
            src, dst = ref.at[direction, pl.ds(1, 4)], ref.at[direction + 2, pl.ds(1, 4)]
        else:
            src, dst = ref.at[direction, :, pl.ds(1, 4)], ref.at[direction + 2, :, pl.ds(1, 4)]
        return pltpu.make_async_remote_copy(
            src_ref=src, dst_ref=dst,
            send_sem=side_send.at[direction, kind], recv_sem=side_recv.at[direction, kind],
            device_id=device, device_id_type=MESH)

    for block in (0, 3):
        for k in (0, 1):
            block_wait(k, block)
    send(0)
    send(1)
    for copy in edge_loads():
        copy.wait()
    for direction, there in ((0, has_west), (1, has_east)):
        @pl.when(there)
        def _():
            side_copy(direction, 0).start()
            side_copy(direction, 1).start()
    for block in (0, 3):
        block_wait(2, block)
    send(2)
    send(3)

    zero = jnp.zeros((8, 128), jnp.float32)
    for there, first in ((has_up, -GHOST), (has_down, ROWS)):
        @pl.when(jnp.logical_not(there))
        def _():
            @pl.loop(0, GHOST)
            def _(i):
                for v in range(NV):
                    for ref in (heat.at[0], heat.at[1], cond, keep):
                        ref[v, at(first) + i] = zero

    def east_row(row):
        c = load(cond, row)
        ce = shift_east(c, lane)
        for v in range(NV):
            east[v, row] = FACE * (c[v] + ce[v])

    def south_row(row):
        for v in range(NV):
            south[v, row] = FACE * (cond[v, row] + cond[v, row + 1])

    def keep_row(row):
        for v in range(NV):
            keep[v, row] = jnp.where(mask[v, row] != 0, 0.0, 1.0)

    for block in (1, 2):
        for k in range(3):
            block_wait(k, block)

    @pl.loop(0, ROWS // 4)
    def _(i):
        for j in range(4):
            row = at(0) + 4 * i + j
            east_row(row)
            keep_row(row)

    @pl.loop(0, ROWS // 4)
    def _(i):
        for j in range(4):
            south_row(at(0) + jnp.minimum(4 * i + j, ROWS - 2))

    def rows_step(time, rows, first=False):
        old, new = heat.at[(time - 1) % 2], heat.at[time % 2]
        above = load(old, rows[0] - 1)
        here = load(old, rows[0])
        north = [south[v, rows[0] - 1] * (here[v] - above[v]) for v in range(NV)]
        for row in rows:
            below = load(old, row + 1)
            down = [south[v, row] * (below[v] - here[v]) for v in range(NV)]
            ahead = shift_east(here, lane)
            flow = [east[v, row] * (ahead[v] - here[v]) for v in range(NV)]
            behind = shift_west(flow, lane)
            for v in range(NV):
                change = (flow[v] - behind[v]) + (down[v] - north[v])
                if first:
                    new[v, row] = jnp.where(mask[v, row] != 0, 1.0, here[v] + change)
                else:
                    new[v, row] = here[v] + keep[v, row] * change
            here, north = below, down

    def sweep(time, low, high, width, first=False):
        count = -(-(high - low) // width)

        @pl.loop(0, count)
        def _(i):
            start = at(jnp.minimum(low + i * width, high - width))
            rows_step(time, [start + j for j in range(width)], first)

    sweep(1, 1, ROWS - 1, 6, first=True)

    for direction, there in ((0, has_east), (1, has_west)):
        @pl.when(there)
        def _():
            side_copy(direction, 0).wait_recv()
            side_copy(direction, 1).wait_recv()
    received(0)
    received(1)
    south_row(at(-1))
    south_row(at(ROWS - 1))
    rows_step(1, [at(0)], first=True)
    rows_step(1, [at(ROWS - 1)], first=True)
    send(6)
    send(7)
    send(4)
    send(5)

    for time in range(2, STEPS + 1):
        level = time - 1
        sweep(time, level, ROWS - level, 6)
        for slot, (_, when) in enumerate(LINES):
            if when == time:
                send(6 + slot)

    received(4)
    received(5)
    shape = (48, 128)
    lane48 = lax.broadcasted_iota(jnp.int32, shape, 1)
    row48 = lax.broadcasted_iota(jnp.int32, shape, 0)
    first_row = jnp.where(has_up, 0, 8)
    end_row = jnp.where(has_down, 48, 40)
    for side in range(2):
        right, left = ((0, 3), (2, 1))[side]
        is_right = lane48 < 64
        first_lane = 0 if side == 0 else jnp.where(has_east, 0, 64)
        end_lane = jnp.where(has_west, 128, 64) if side == 0 else 128
        exists = ((row48 >= first_row) & (row48 < end_row)
                  & (lane48 >= first_lane) & (lane48 < end_lane))

        def pick(k):
            value = jnp.where(is_right, edge_fc[right, k].reshape(shape),
                              edge_fc[left, k].reshape(shape))
            return jnp.where(exists, value, 0.0)

        f = pick(0)
        c = pick(1)
        source = jnp.where(is_right, edge_m[right].reshape(shape),
                           edge_m[left].reshape(shape)) != 0
        source = jnp.logical_and(source, exists)
        stay = jnp.where(jnp.logical_and(exists, jnp.logical_not(source)), 1.0, 0.0)
        turns = ((127, 1), (1, 1), (47, 0), (1, 0))
        faces = [stay * (FACE * (c + pltpu.roll(c, *turn))) for turn in turns]

        def substep(f):
            total = f
            for turn, face in zip(turns, faces):
                total = total + face * (pltpu.roll(f, *turn) - f)
            return total

        f = jnp.where(source, 1.0, substep(f))
        f = lax.fori_loop(1, STEPS, lambda _, x: substep(x), f)
        edge_out[side] = f[8:40]

    received(2)
    received(3)
    for there, rows in ((has_up, (-3, -2, -1)), (has_down, (ROWS, ROWS + 1, ROWS + 2))):
        for row in rows:
            east_row(at(row))

        @pl.when(there)
        def _():
            for row in rows:
                keep_row(at(row))
    for row in (-4, -3, -2, ROWS, ROWS + 1, ROWS + 2):
        south_row(at(row))

    for slot in range(13):
        sent(slot)
    for slot in range(6, 13):
        received(slot)
    for time in range(2, STEPS + 1):
        level = time - 1
        out_by = min(level, 7 - level)
        top = [at(row) for row in range(-out_by, level)]
        bottom = [at(row) for row in range(ROWS - level, ROWS + out_by)]
        rows_step(time, top)
        rows_step(time, bottom)

    sub = lax.broadcasted_iota(jnp.int32, (8, 128), 0)
    final = heat.at[STEPS % 2]
    first_columns = jnp.logical_and(sub == 0, lane < 8)
    last_columns = jnp.logical_and(sub == 7, lane >= 120)

    @pl.loop(0, ROWS // 8)
    def _(i):
        for j in range(8):
            row = 8 * i + j
            for side, v, where in ((0, 0, first_columns), (1, NV - 1, last_columns)):
                patch = jnp.broadcast_to(edge_out[side, pl.ds(row, 1), :], (8, 128))
                final[v, at(row)] = jnp.where(where, patch, final[v, at(row)])

    def store(block, s):
        return pltpu.make_async_copy(
            final.at[:, pl.ds(at(8 * block), 8), s, :], out.at[block, s], out_sem.at[block, s])

    for block in range(4):
        for s in range(8):
            store(block, s).start()
    for block in range(4):
        for s in range(8):
            store(block, s).wait()
    for direction, there in ((0, has_west), (1, has_east)):
        @pl.when(there)
        def _():
            side_copy(direction, 0).wait_send()
            side_copy(direction, 1).wait_send()


def tiles(x):
    return x.reshape(4, 8, 8, NV, 128).transpose(0, 2, 3, 1, 4)


def shards(starting_warmth, diffusivity_field, emitter_mask):
    wide = ROWS + 2 * GHOST
    result = pl.pallas_call(
        kernel,
        out_shape=jax.ShapeDtypeStruct((4, 8, NV, 8, 128), jnp.float32),
        in_specs=[pl.BlockSpec(memory_space=pl.ANY)] * 3,
        out_specs=pl.BlockSpec(memory_space=pl.ANY),
        scratch_shapes=[
            pltpu.VMEM((2, NV, wide, 8, 128), jnp.float32),
            pltpu.VMEM((NV, wide, 8, 128), jnp.float32),
            pltpu.VMEM((NV, wide, 8, 128), jnp.int32),
            pltpu.VMEM((NV, wide, 8, 128), jnp.float32),
            pltpu.VMEM((NV, wide, 8, 128), jnp.float32),
            pltpu.VMEM((NV, wide, 8, 128), jnp.float32),
            pltpu.VMEM((4, 2, 6, 8, 128), jnp.float32),
            pltpu.VMEM((4, 6, 8, 128), jnp.int32),
            pltpu.VMEM((2, ROWS, 128), jnp.float32),
            pltpu.SemaphoreType.DMA((3, 4)),
            pltpu.SemaphoreType.DMA((6,)),
            pltpu.SemaphoreType.DMA((2, 13)),
            pltpu.SemaphoreType.DMA((2, 13)),
            pltpu.SemaphoreType.DMA((2, 2)),
            pltpu.SemaphoreType.DMA((2, 2)),
            pltpu.SemaphoreType.DMA((4, 8)),
        ],
        compiler_params=pltpu.CompilerParams(
            collective_id=0, has_side_effects=True, vmem_limit_bytes=60 * 2**20),
    )(tiles(starting_warmth), tiles(diffusivity_field), tiles(emitter_mask))
    return result.transpose(0, 3, 1, 2, 4).reshape(ROWS, 128 * 128)


def solution(mesh):
    return jax.shard_map(
        shards,
        mesh=mesh,
        in_specs=(P("tile", "seg"),) * 3,
        out_specs=P("tile", "seg"),
        check_vma=False,
    )
```

time: 200 us -> 37.1 us (0.19); the launches traced: 198 us -> 37 us
  other arithmetic: 65.3 us -> 0 us
  starting transfers between devices: 59.6 us -> 0 us
  waiting for transfers between devices: 34.6 us -> 0 us
  local copies, waits for them, and re-layouts: 37.6 us -> 3.05 us
  Pallas kernels: 0 us -> 33.9 us
    ppermute x20 -> x0, starting transfers between devices: 59.6 us -> none  [the longest x10 39.6 us: padded(): before = lax.ppermute(last, axis, up)]
    ppermute x20 -> x0, waiting for transfers between devices: 34.6 us -> none  [the longest x10 30.4 us: padded(): after = lax.ppermute(first, axis, down)]
    pallas_call x0 -> x1, Pallas kernels: none -> 33.9 us  [shards(): pl.pallas_call(kernel, out_shape=jax.ShapeDtypeStruct((4, 8, NV, 8, 128),...]
    mul x4 -> x0, other arithmetic: 27.4 us -> none  [advance(): updated = updated * interior_region]
    select_n x4 -> x0, other arithmetic: 27.2 us -> none  [advance(): updated = jnp.where(source, jnp.float32(1.0), updated)]
    concatenate x5 -> x0, local copies, waits for them, and re-layouts: 22.9 us -> none  [padded(): shard = jnp.concatenate([before, shard, after], axis=dim)]
    slice x9 -> x0, local copies, waits for them, and re-layouts: 8.16 us -> none  [the longest x5 6.99 us: padded(): last = lax.slice_in_dim(shard, length - width, length, axis=dim)]
    concatenate x5 -> x0, other arithmetic: 6.63 us -> none  [padded(): shard = jnp.concatenate([before, shard, after], axis=dim)]
  transfers between devices with their start and end apart: 20 -> 0, of which waited for: 8 -> 0; matrix products, arithmetic and copies ran while one was open for 9% -> 0% of each run, Pallas kernels for 0% -> 0%
where the time goes in v1:
time: 37.1 us; the launch traced here: 37 us
  Pallas kernels  33.9 us (91%)
  local copies, waits for them, and re-layouts  3.05 us (8%)
    pallas_call x1, Pallas kernels, shards(): pl.pallas_call(kernel, out_shape=jax.ShapeDtypeStruct((4, 8, NV, 8, 128),...  33.9 us
    unnamed x1, local copies, waits for them, and re-layouts  3.05 us

profile of v1, /device:TPU:111, one launch (start us, length us, event | category | flops | bytes accessed | tf_op | source)
XLA Modules:
  0.0 37.0 jit_solution(7004977183143172327)
XLA Ops:
  0.0 33.9 %shard_map.37 = f32[4,8,16,8,128]{4,3,2,1,0:T(8,128)} custom-call(f32[4,8,16,8,128]{4,3,2,1,0:T(8,128)} %bitcast.13, f32[4,8,16,8,128]{4,3,2,1,0:T(8,128)} %bitcast.14, s32[4,8,16,8,128]{4,3,2,1,0:T(8,128)} %bitcast.15), custom_call_target="tpu_custom_call" | custom-call | tf_op jit(solution)/shard_map/pallas_call | solution.py:377
  33.9 3.0 %copy.5 = f32[32,16384]{1,0:T(8,128)} copy(f32[32,16384]{1,0:T(8,128)} %bitcast.12) | data formatting | bytes 4194304

commit v2 on v1

v2 whole, which is shorter than its diff:
```python
import functools

import jax
import jax.numpy as jnp
from jax import lax
from jax.experimental import pallas as pl
from jax.experimental.pallas import tpu as pltpu
from jax.sharding import PartitionSpec as P

STEPS = 8
FACE = 0.24 * 0.5
ROWS = 32
GHOST = 4
NV = 16
LOW, HIGH = 7, 25
MESH = pl.DeviceIdType.MESH

LINES = ((1, 1), (2, 1), (2, 2), (3, 2), (3, 3), (4, 3), (4, 4))


def at(row):
    return row + GHOST


def reg(v):
    return pl.ds(8 * v, 8)


def load(ref, row):
    return [ref[row, reg(v), :] for v in range(NV)]


def position():
    return (lax.broadcasted_iota(jnp.int32, (8, 128), 0),
            lax.broadcasted_iota(jnp.int32, (8, 128), 1))


def after_last(first):
    sub, _ = position()
    down = pltpu.roll(first, 7, 0)
    return jnp.where(sub == 7, pltpu.roll(down, 127, 1), down)


def before_first(last):
    sub, _ = position()
    up = pltpu.roll(last, 1, 0)
    return jnp.where(sub == 0, pltpu.roll(up, 1, 1), up)


def comb(j):
    return pl.ds(64 * (j % 2) + j // 2, 8, stride=8)


def spread(x, ref, row):
    turned = x.T
    for j in range(NV):
        ref[row, comb(j), :] = turned[8 * j:8 * j + 8]


def gather(ref, row):
    return jnp.concatenate([ref[row, comb(j), :] for j in range(NV)], axis=0).T


def finish(ref, at_row, edge, row, put):
    sub, lane = position()
    x = gather(ref, at_row)
    for side, first, where in ((0, 0, (sub == 0) & (lane < 8)),
                               (1, 120, (sub == 7) & (lane >= 120))):
        patch = jnp.broadcast_to(edge[side, pl.ds(row, 1), :], (8, 128))
        put(pl.ds(first, 8), jnp.where(where, patch, x[first:first + 8]))
    put(pl.ds(8, 112), x[8:120])


def kernel(
    f_in, c_in, m_in,
    ready, border, edge_out,
    f_rows, c_rows, m_rows, heat, cond, east, west, south, keep,
    edge_fc, edge_m,
    load_sem, edge_load_sem, send_sem, recv_sem, side_send, side_recv,
):
    tile = lax.axis_index("tile")
    seg = lax.axis_index("seg")
    n_tile = lax.axis_size("tile")
    n_seg = lax.axis_size("seg")
    has_up = tile > 0
    has_down = tile < n_tile - 1
    has_west = seg > 0
    has_east = seg < n_seg - 1

    def edge_loads():
        copies = []
        for piece, block in enumerate((0, 127)):
            for k, src in enumerate((f_in, c_in)):
                copies.append(pltpu.make_async_copy(
                    src.at[:, block], edge_fc.at[piece, k, pl.ds(1, 4)],
                    edge_load_sem.at[3 * piece + k]))
            copies.append(pltpu.make_async_copy(
                m_in.at[:, block], edge_m.at[piece, pl.ds(1, 4)],
                edge_load_sem.at[3 * piece + 2]))
        return copies

    arrays = ((f_in, f_rows), (c_in, c_rows), (m_in, m_rows))
    groups = ((0, 31), (1, 2, 3, 28, 29, 30), tuple(range(4, 28)))

    def start_loads(k, group):
        src, dst = arrays[k]
        for row in groups[group]:
            pltpu.make_async_copy(
                src.at[row // 8, :, row % 8], dst.at[row], load_sem.at[k, group]).start()

    def wait_loads(k, group):
        dst = arrays[k][1].at[pl.ds(0, len(groups[group]))]
        pltpu.make_async_copy(dst, dst, load_sem.at[k, group]).wait()

    for k in range(3):
        start_loads(k, 0)
    for copy in edge_loads():
        copy.start()
    for group in (1, 2):
        for k in (1, 2, 0):
            start_loads(k, group)

    barrier = pltpu.get_barrier_semaphore()
    sides = (
        (has_up, {"tile": tile - 1}), (has_down, {"tile": tile + 1}),
        (has_west, {"seg": seg - 1}), (has_east, {"seg": seg + 1}),
    )
    for there, device in sides:
        @pl.when(there)
        def _():
            pl.semaphore_signal(barrier, inc=1, device_id=device, device_id_type=MESH)
    count = sum(there.astype(jnp.int32) for there, _ in sides)
    pl.semaphore_wait(barrier, count)

    def rows_of(direction, near, far):
        if direction == 0:
            return near - 1, ROWS + near - 1, far - near + 1
        return ROWS - far, -far, far - near + 1

    def remote(direction, slot, src, dst):
        device = {"tile": tile - 1 if direction == 0 else tile + 1}
        return pltpu.make_async_remote_copy(
            src_ref=src, dst_ref=dst,
            send_sem=send_sem.at[direction, slot], recv_sem=recv_sem.at[direction, slot],
            device_id=device, device_id_type=MESH)

    def tile_copy(direction, slot):
        if slot == 0:
            ref, near, far = heat.at[0], 1, 1
        elif slot == 1:
            ref, near, far = cond, 1, 1
        elif slot == 2:
            ref, near, far = cond, 2, 4
        elif slot == 3:
            ref, near, far = keep, 1, 3
        elif slot < 6:
            block = 1 if direction == 0 else 4
            land = 5 if direction == 0 else 0
            if slot == 4:
                return remote(direction, slot, edge_fc.at[:, :, block], edge_fc.at[:, :, land])
            return remote(direction, slot, edge_m.at[:, block], edge_m.at[:, land])
        else:
            distance, time = LINES[slot - 6]
            ref, near, far = heat.at[time % 2], distance, distance
        src, dst, count = rows_of(direction, near, far)
        return remote(direction, slot, ref.at[pl.ds(at(src), count)],
                      ref.at[pl.ds(at(dst), count)])

    def send(slot):
        for direction, there in ((0, has_up), (1, has_down)):
            @pl.when(there)
            def _():
                tile_copy(direction, slot).start()

    def sent(slot):
        for direction, there in ((0, has_up), (1, has_down)):
            @pl.when(there)
            def _():
                tile_copy(direction, slot).wait_send()

    def received(slot):
        for direction, there in ((0, has_down), (1, has_up)):
            @pl.when(there)
            def _():
                tile_copy(direction, slot).wait_recv()

    def side_copy(direction, kind):
        device = {"seg": seg - 1 if direction == 0 else seg + 1}
        ref = edge_m if kind else edge_fc
        if kind:
            src, dst = ref.at[direction, pl.ds(1, 4)], ref.at[direction + 2, pl.ds(1, 4)]
        else:
            src, dst = ref.at[direction, :, pl.ds(1, 4)], ref.at[direction + 2, :, pl.ds(1, 4)]
        return pltpu.make_async_remote_copy(
            src_ref=src, dst_ref=dst,
            send_sem=side_send.at[direction, kind], recv_sem=side_recv.at[direction, kind],
            device_id=device, device_id_type=MESH)

    def spread_heat(row):
        spread(f_rows[row], heat.at[0], at(row))

    def spread_fixed(row):
        spread(jnp.where(m_rows[row] != 0, -c_rows[row], c_rows[row]), cond, at(row))
        for v in range(NV):
            both = cond[at(row), reg(v), :]
            keep[at(row), reg(v), :] = jnp.where(both < 0.0, 0.0, 1.0)
            cond[at(row), reg(v), :] = jnp.abs(both)

    for copy in edge_loads():
        copy.wait()
    for direction, there in ((0, has_west), (1, has_east)):
        @pl.when(there)
        def _():
            side_copy(direction, 0).start()
            side_copy(direction, 1).start()
    for k in range(3):
        wait_loads(k, 0)
    for row in groups[0]:
        spread_heat(row)
        spread_fixed(row)
    send(0)
    send(1)
    for k in range(3):
        wait_loads(k, 1)

    @pl.loop(0, 2)
    def _(i):
        for j in range(3):
            spread_fixed(1 + 27 * i + j)

    send(2)
    send(3)

    zero = jnp.zeros((8, 128), jnp.float32)
    for there, first in ((has_up, -GHOST), (has_down, ROWS)):
        @pl.when(jnp.logical_not(there))
        def _():
            @pl.loop(0, GHOST)
            def _(i):
                for v in range(NV):
                    for ref in (heat.at[0], heat.at[1], cond, keep):
                        ref[at(first) + i, reg(v), :] = zero

    def east_row(row):
        c = load(cond, row)
        c.append(after_last(c[0]))
        for v in range(NV):
            face = FACE * (c[v] + c[v + 1])
            east[row, reg(v), :] = face
        west[row] = before_first(face)

    def south_row(row):
        for v in range(NV):
            south[row, reg(v), :] = FACE * (
                cond[row, reg(v), :] + cond[row + 1, reg(v), :])

    @pl.loop(0, 2)
    def _(i):
        for j in range(3):
            spread_heat(1 + 27 * i + j)

    for k in range(3):
        wait_loads(k, 2)

    @pl.loop(0, 12)
    def _(i):
        for j in range(2):
            spread_fixed(4 + 2 * i + j)
            spread_heat(4 + 2 * i + j)

    @pl.loop(0, ROWS // 4)
    def _(i):
        for j in range(4):
            east_row(at(0) + 4 * i + j)

    @pl.loop(0, ROWS // 4)
    def _(i):
        for j in range(4):
            south_row(at(0) + jnp.minimum(4 * i + j, ROWS - 2))

    def rows_step(time, rows, first=False, put=None):
        old, new = heat.at[(time - 1) % 2], heat.at[time % 2]
        above = load(old, rows[0] - 1)
        here = load(old, rows[0])
        north = [south[rows[0] - 1, reg(v), :] * (here[v] - above[v]) for v in range(NV)]
        for i, row in enumerate(rows):
            below = load(old, row + 1)
            ahead = here[1:] + [after_last(here[0])]
            behind = west[row] * (here[0] - before_first(here[-1]))
            down = []
            for v in range(NV):
                down.append(south[row, reg(v), :] * (below[v] - here[v]))
                flow = east[row, reg(v), :] * (ahead[v] - here[v])
                change = (flow - behind) + (down[v] - north[v])
                behind = flow
                if first:
                    value = jnp.where(keep[row, reg(v), :] == 0.0, 1.0, here[v] + change)
                else:
                    value = here[v] + keep[row, reg(v), :] * change
                if put is None:
                    new[row, reg(v), :] = value
                else:
                    put(i, v, value)
            here, north = below, down

    def sweep(time, low, high, width, first=False):
        count = -(-(high - low) // width)

        @pl.loop(0, count)
        def _(i):
            start = at(jnp.minimum(low + i * width, high - width))
            rows_step(time, [start + j for j in range(width)], first)

    sweep(1, 1, ROWS - 1, 6, first=True)

    for direction, there in ((0, has_east), (1, has_west)):
        @pl.when(there)
        def _():
            side_copy(direction, 0).wait_recv()
            side_copy(direction, 1).wait_recv()
    received(0)
    received(1)
    south_row(at(-1))
    south_row(at(ROWS - 1))
    rows_step(1, [at(0)], first=True)
    rows_step(1, [at(ROWS - 1)], first=True)
    send(6)
    send(7)
    send(4)
    send(5)

    for time in range(2, STEPS + 1):
        level = time - 1
        sweep(time, level, ROWS - level, 6)
        for slot, (_, when) in enumerate(LINES):
            if when == time:
                send(6 + slot)

    received(4)
    received(5)
    shape = (48, 128)
    lane48 = lax.broadcasted_iota(jnp.int32, shape, 1)
    row48 = lax.broadcasted_iota(jnp.int32, shape, 0)
    first_row = jnp.where(has_up, 0, 8)
    end_row = jnp.where(has_down, 48, 40)
    turns = ((127, 1), (1, 1), (47, 0), (1, 0))

    def substep(f, faces):
        total = f
        for turn, face in zip(turns, faces):
            total = total + face * (pltpu.roll(f, *turn) - f)
        return total

    starts, all_faces = [], []
    for side in range(2):
        right, left = ((0, 3), (2, 1))[side]
        is_right = lane48 < 64
        first_lane = 0 if side == 0 else jnp.where(has_east, 0, 64)
        end_lane = jnp.where(has_west, 128, 64) if side == 0 else 128
        exists = ((row48 >= first_row) & (row48 < end_row)
                  & (lane48 >= first_lane) & (lane48 < end_lane))

        def pick(k):
            value = jnp.where(is_right, edge_fc[right, k].reshape(shape),
                              edge_fc[left, k].reshape(shape))
            return jnp.where(exists, value, 0.0)

        f = pick(0)
        c = pick(1)
        source = jnp.where(is_right, edge_m[right].reshape(shape),
                           edge_m[left].reshape(shape)) != 0
        source = jnp.logical_and(source, exists)
        stay = jnp.where(jnp.logical_and(exists, jnp.logical_not(source)), 1.0, 0.0)
        faces = [stay * (FACE * (c + pltpu.roll(c, *turn))) for turn in turns]
        starts.append(jnp.where(source, 1.0, substep(f, faces)))
        all_faces.append(faces)

    ends = lax.fori_loop(
        1, STEPS,
        lambda _, fs: tuple(substep(f, faces) for f, faces in zip(fs, all_faces)),
        tuple(starts))
    for side in range(2):
        edge_out[side] = ends[side][8:40]

    @pl.loop(LOW, HIGH)
    def _(row):
        def put(where, value):
            ready[row, where, :] = value

        finish(heat.at[STEPS % 2], at(row), edge_out, row, put)

    received(2)
    received(3)
    for row in (-3, -2, -1, ROWS, ROWS + 1, ROWS + 2):
        east_row(at(row))

    for row in (-4, -3, -2, ROWS, ROWS + 1, ROWS + 2):
        south_row(at(row))

    for slot in range(13):
        sent(slot)
    for slot in range(6, 13):
        received(slot)
    for time in range(2, STEPS + 1):
        level = time - 1
        out_by = min(level, 7 - level)
        top = [at(row) for row in range(-out_by, level)]
        bottom = [at(row) for row in range(ROWS - level, ROWS + out_by)]
        for half, rows in enumerate((top, bottom)):
            put = None
            if time == STEPS:
                def put(i, v, value, half=half):
                    border[LOW * half + i, reg(v), :] = value
            rows_step(time, rows, put=put)
    for direction, there in ((0, has_west), (1, has_east)):
        @pl.when(there)
        def _():
            side_copy(direction, 0).wait_send()
            side_copy(direction, 1).wait_send()


def write(ready, border, edge, out, rest, sem):
    def copy(src, row, slot):
        return pltpu.make_async_copy(src, out.at[row // 8, :, row % 8], sem.at[slot])

    last = [(i, i if i < LOW else HIGH + i - LOW) for i in range(2 * LOW)]
    for row in range(LOW, HIGH):
        copy(ready.at[row], row, row).start()
    for i, row in last:
        def put(where, value):
            rest[i, where, :] = value

        finish(border, i, edge, row, put)
        copy(rest.at[i], row, row).start()
    for row in range(LOW, HIGH):
        copy(ready.at[row], row, row).wait()
    for i, row in last:
        copy(rest.at[i], row, row).wait()


def tiles(x):
    return x.reshape(4, 8, 128, 128).transpose(0, 2, 1, 3)


def shards(starting_warmth, diffusivity_field, emitter_mask):
    wide = ROWS + 2 * GHOST
    values = (128, 128)
    inside = pl.BlockSpec(memory_space=pltpu.VMEM)
    outside = pl.BlockSpec(memory_space=pltpu.HBM)
    ready, border, edge = pl.pallas_call(
        kernel,
        out_shape=(
            jax.ShapeDtypeStruct((ROWS, 128, 128), jnp.float32),
            jax.ShapeDtypeStruct((2 * LOW, *values), jnp.float32),
            jax.ShapeDtypeStruct((2, ROWS, 128), jnp.float32),
        ),
        in_specs=[outside] * 3,
        out_specs=(inside,) * 3,
        scratch_shapes=[
            pltpu.VMEM((ROWS, 128, 128), jnp.float32),
            pltpu.VMEM((ROWS, 128, 128), jnp.float32),
            pltpu.VMEM((ROWS, 128, 128), jnp.int32),
            pltpu.VMEM((2, wide, *values), jnp.float32),
            pltpu.VMEM((wide, *values), jnp.float32),
            pltpu.VMEM((wide, *values), jnp.float32),
            pltpu.VMEM((wide, 8, 128), jnp.float32),
            pltpu.VMEM((wide, *values), jnp.float32),
            pltpu.VMEM((wide, *values), jnp.float32),
            pltpu.VMEM((4, 2, 6, 8, 128), jnp.float32),
            pltpu.VMEM((4, 6, 8, 128), jnp.int32),
            pltpu.SemaphoreType.DMA((3, 3)),
            pltpu.SemaphoreType.DMA((6,)),
            pltpu.SemaphoreType.DMA((2, 13)),
            pltpu.SemaphoreType.DMA((2, 13)),
            pltpu.SemaphoreType.DMA((2, 2)),
            pltpu.SemaphoreType.DMA((2, 2)),
        ],
        compiler_params=pltpu.CompilerParams(
            collective_id=0, has_side_effects=True, vmem_limit_bytes=50 * 2**20),
    )(tiles(starting_warmth), tiles(diffusivity_field), tiles(emitter_mask))
    result = pl.pallas_call(
        write,
        out_shape=jax.ShapeDtypeStruct((4, 128, 8, 128), jnp.float32),
        in_specs=[inside] * 3,
        out_specs=outside,
        scratch_shapes=[
            pltpu.VMEM((2 * LOW, 128, 128), jnp.float32),
            pltpu.SemaphoreType.DMA((ROWS,)),
        ],
        compiler_params=pltpu.CompilerParams(vmem_limit_bytes=16 * 2**20),
    )(ready, border, edge)
    return result.transpose(0, 2, 1, 3).reshape(ROWS, 128 * 128)


def solution(mesh):
    return jax.shard_map(
        shards,
        mesh=mesh,
        in_specs=(P("tile", "seg"),) * 3,
        out_specs=P("tile", "seg"),
        check_vma=False,
    )
```

time: 37.1 us -> 22.6 us (0.61)
  Pallas kernels: 33.9 us -> 22.5 us
  local copies, waits for them, and re-layouts: 3.05 us -> 0 us
    pallas_call x1 -> x2, Pallas kernels: 33.9 us -> 22.5 us  [the longest x1 20.9 us: shards(): pl.pallas_call(kernel, out_shape=(jax.ShapeDtypeStruct((ROWS, 128, 128),...]
    unnamed x1 -> x0, local copies, waits for them, and re-layouts: 3.05 us -> none
where the time goes in v2:
time: 22.6 us; the launch traced here: 22.5 us
  Pallas kernels  22.5 us (100%)
    pallas_call x1, Pallas kernels, shards(): pl.pallas_call(kernel, out_shape=(jax.ShapeDtypeStruct((ROWS, 128, 128),...  20.9 us
    pallas_call x1, Pallas kernels, shards(): pl.pallas_call(write, out_shape=jax.ShapeDtypeStruct((4, 128, 8, 128), jn...  1.6 us

profile of v2, /device:TPU:111, one launch (start us, length us, event | category | flops | bytes accessed | tf_op | source)
XLA Modules:
  0.0 22.5 jit_solution(3826433485332781027)
XLA Ops:
  0.0 20.9 %shard_map.37 = (f32[32,128,128]{2,1,0:T(8,128)S(1)}, f32[14,128,128]{2,1,0:T(8,128)S(1)}, f32[2,32,128]{2,1,0:T(8,128)S(1)}) custom-call(f32[4,128,8,128]{3,2,1,0:T(8,128)} %bitcast.12, f32[4,128,8,128]{3,2,1,0:T(8,128)} %bitcast.13, s32[4,128,8,128]{3,2,1,0:T(8,128)} %bitcast.14), custom_call_target="tpu_custom_call" | custom-call | tf_op jit(solution)/shard_map/pallas_call | solution.py:450
  20.9 1.6 %shard_map.38 = f32[4,128,8,128]{3,2,1,0:T(8,128)} custom-call(f32[32,128,128]{2,1,0:T(8,128)S(1)} %get-tuple-element.8.ready, f32[14,128,128]{2,1,0:T(8,128)S(1)} %get-tuple-element.9.border, f32[2,32,128]{2,1,0:T(8,128)S(1)} %get-tuple-element.10.edge), custom_call_target="tpu_custom_call" | custom-call | tf_op jit(solution)/shard_map/pallas_call | solution.py:481

commit v3 on v2

--- a/solution.py
+++ b/solution.py
@@ -15,7 +15,9 @@
 LOW, HIGH = 7, 25
 MESH = pl.DeviceIdType.MESH
 
-LINES = ((1, 1), (2, 1), (2, 2), (3, 2), (3, 3), (4, 3), (4, 4))
+LINES = ((1, 2), (2, 3), (3, 4), (4, 4))
+SLOTS = 6 + len(LINES)
+FILLS = (((6, 7), 1, 4), ((8,), 5, 6), ((9,), 7, 7))
 
 
 def at(row):
@@ -87,6 +89,17 @@
     has_west = seg > 0
     has_east = seg < n_seg - 1
 
+    barrier = pltpu.get_barrier_semaphore()
+    sides = (
+        (has_up, {"tile": tile - 1}), (has_down, {"tile": tile + 1}),
+        (has_west, {"seg": seg - 1}), (has_east, {"seg": seg + 1}),
+    )
+    for there, device in sides:
+        @pl.when(there)
+        def _():
+            pl.semaphore_signal(barrier, inc=1, device_id=device, device_id_type=MESH)
+    count = sum(there.astype(jnp.int32) for there, _ in sides)
+
     def edge_loads():
         copies = []
         for piece, block in enumerate((0, 127)):
@@ -114,22 +127,11 @@
 
     for k in range(3):
         start_loads(k, 0)
+    for k in (1, 2):
+        start_loads(k, 1)
     for copy in edge_loads():
         copy.start()
-    for group in (1, 2):
-        for k in (1, 2, 0):
-            start_loads(k, group)
-
-    barrier = pltpu.get_barrier_semaphore()
-    sides = (
-        (has_up, {"tile": tile - 1}), (has_down, {"tile": tile + 1}),
-        (has_west, {"seg": seg - 1}), (has_east, {"seg": seg + 1}),
-    )
-    for there, device in sides:
-        @pl.when(there)
-        def _():
-            pl.semaphore_signal(barrier, inc=1, device_id=device, device_id_type=MESH)
-    count = sum(there.astype(jnp.int32) for there, _ in sides)
+
     pl.semaphore_wait(barrier, count)
 
     def rows_of(direction, near, far):
@@ -160,8 +162,8 @@
                 return remote(direction, slot, edge_fc.at[:, :, block], edge_fc.at[:, :, land])
             return remote(direction, slot, edge_m.at[:, block], edge_m.at[:, land])
         else:
-            distance, time = LINES[slot - 6]
-            ref, near, far = heat.at[time % 2], distance, distance
+            near, far = LINES[slot - 6]
+            ref = heat.at[(slot - 5) % 2]
         src, dst, count = rows_of(direction, near, far)
         return remote(direction, slot, ref.at[pl.ds(at(src), count)],
                       ref.at[pl.ds(at(dst), count)])
@@ -171,6 +173,19 @@
             @pl.when(there)
             def _():
                 tile_copy(direction, slot).start()
+
+    first_core = tile % 2 == 0
+
+    def send_far(slot):
+        for direction, there in ((0, has_up), (1, has_down & jnp.logical_not(first_core))):
+            @pl.when(there)
+            def _():
+                tile_copy(direction, slot).start()
+
+    def send_near(slot):
+        @pl.when(has_down & first_core)
+        def _():
+            tile_copy(1, slot).start()
 
     def sent(slot):
         for direction, there in ((0, has_up), (1, has_down)):
@@ -206,6 +221,16 @@
             keep[at(row), reg(v), :] = jnp.where(both < 0.0, 0.0, 1.0)
             cond[at(row), reg(v), :] = jnp.abs(both)
 
+    for k in range(3):
+        wait_loads(k, 0)
+    start_loads(0, 1)
+    for k in (0, 1, 2):
+        start_loads(k, 2)
+    for row in groups[0]:
+        spread_heat(row)
+        spread_fixed(row)
+    send(0)
+    send(1)
     for copy in edge_loads():
         copy.wait()
     for direction, there in ((0, has_west), (1, has_east)):
@@ -213,14 +238,7 @@
         def _():
             side_copy(direction, 0).start()
             side_copy(direction, 1).start()
-    for k in range(3):
-        wait_loads(k, 0)
-    for row in groups[0]:
-        spread_heat(row)
-        spread_fixed(row)
-    send(0)
-    send(1)
-    for k in range(3):
+    for k in (1, 2):
         wait_loads(k, 1)
 
     @pl.loop(0, 2)
@@ -254,6 +272,8 @@
             south[row, reg(v), :] = FACE * (
                 cond[row, reg(v), :] + cond[row + 1, reg(v), :])
 
+    wait_loads(0, 1)
+
     @pl.loop(0, 2)
     def _(i):
         for j in range(3):
@@ -268,17 +288,7 @@
             spread_fixed(4 + 2 * i + j)
             spread_heat(4 + 2 * i + j)
 
-    @pl.loop(0, ROWS // 4)
-    def _(i):
-        for j in range(4):
-            east_row(at(0) + 4 * i + j)
-
-    @pl.loop(0, ROWS // 4)
-    def _(i):
-        for j in range(4):
-            south_row(at(0) + jnp.minimum(4 * i + j, ROWS - 2))
-
-    def rows_step(time, rows, first=False, put=None):
+    def rows_step(time, rows, put=None):
         old, new = heat.at[(time - 1) % 2], heat.at[time % 2]
         above = load(old, rows[0] - 1)
         here = load(old, rows[0])
@@ -293,25 +303,55 @@
                 flow = east[row, reg(v), :] * (ahead[v] - here[v])
                 change = (flow - behind) + (down[v] - north[v])
                 behind = flow
-                if first:
-                    value = jnp.where(keep[row, reg(v), :] == 0.0, 1.0, here[v] + change)
-                else:
-                    value = here[v] + keep[row, reg(v), :] * change
+                value = here[v] + keep[row, reg(v), :] * change
                 if put is None:
                     new[row, reg(v), :] = value
                 else:
                     put(i, v, value)
             here, north = below, down
 
-    def sweep(time, low, high, width, first=False):
+    def sweep(time, low, high, width):
         count = -(-(high - low) // width)
 
         @pl.loop(0, count)
         def _(i):
             start = at(jnp.minimum(low + i * width, high - width))
-            rows_step(time, [start + j for j in range(width)], first)
-
-    sweep(1, 1, ROWS - 1, 6, first=True)
+            rows_step(time, [start + j for j in range(width)])
+
+    def first_step(rows):
+        old, new = heat.at[0], heat.at[1]
+        above, here = load(old, rows[0] - 1), load(old, rows[0])
+        c_above, c = load(cond, rows[0] - 1), load(cond, rows[0])
+        north = []
+        for v in range(NV):
+            face = FACE * (c_above[v] + c[v])
+            south[rows[0] - 1, reg(v), :] = face
+            north.append(face * (here[v] - above[v]))
+        for row in rows:
+            below, c_below = load(old, row + 1), load(cond, row + 1)
+            ahead = here[1:] + [after_last(here[0])]
+            c_ahead = c[1:] + [after_last(c[0])]
+            face = FACE * (c[-1] + c_ahead[-1])
+            west_face = before_first(face)
+            west[row] = west_face
+            behind = west_face * (here[0] - before_first(here[-1]))
+            down = []
+            for v in range(NV):
+                face = FACE * (c[v] + c_below[v])
+                south[row, reg(v), :] = face
+                down.append(face * (below[v] - here[v]))
+                face = FACE * (c[v] + c_ahead[v])
+                east[row, reg(v), :] = face
+                flow = face * (ahead[v] - here[v])
+                change = (flow - behind) + (down[v] - north[v])
+                behind = flow
+                new[row, reg(v), :] = jnp.where(
+                    keep[row, reg(v), :] == 0.0, 1.0, here[v] + change)
+            here, north, c = below, down, c_below
+
+    @pl.loop(0, (ROWS - 2) // 3)
+    def _(i):
+        first_step([at(1) + 3 * i + j for j in range(3)])
 
     for direction, there in ((0, has_east), (1, has_west)):
         @pl.when(there)
@@ -320,21 +360,20 @@
             side_copy(direction, 1).wait_recv()
     received(0)
     received(1)
-    south_row(at(-1))
-    south_row(at(ROWS - 1))
-    rows_step(1, [at(0)], first=True)
-    rows_step(1, [at(ROWS - 1)], first=True)
-    send(6)
-    send(7)
+    first_step([at(0)])
+    first_step([at(ROWS - 1)])
+    send_far(6)
     send(4)
     send(5)
 
     for time in range(2, STEPS + 1):
         level = time - 1
         sweep(time, level, ROWS - level, 6)
-        for slot, (_, when) in enumerate(LINES):
-            if when == time:
-                send(6 + slot)
+        if time <= len(LINES):
+            send_far(5 + time)
+        if time == len(LINES):
+            for slot in range(6, SLOTS):
+                send_near(slot)
 
     received(4)
     received(5)
@@ -382,12 +421,15 @@
     for side in range(2):
         edge_out[side] = ends[side][8:40]
 
-    @pl.loop(LOW, HIGH)
-    def _(row):
-        def put(where, value):
-            ready[row, where, :] = value
-
-        finish(heat.at[STEPS % 2], at(row), edge_out, row, put)
+    @pl.loop(0, 3)
+    def _(i):
+        for j in range(6):
+            row = LOW + 6 * i + j
+
+            def put(where, value, row=row):
+                ready[row, where, :] = value
+
+            finish(heat.at[STEPS % 2], at(row), edge_out, row, put)
 
     received(2)
     received(3)
@@ -397,21 +439,23 @@
     for row in (-4, -3, -2, ROWS, ROWS + 1, ROWS + 2):
         south_row(at(row))
 
-    for slot in range(13):
+    for slot in range(SLOTS):
         sent(slot)
-    for slot in range(6, 13):
-        received(slot)
-    for time in range(2, STEPS + 1):
-        level = time - 1
-        out_by = min(level, 7 - level)
-        top = [at(row) for row in range(-out_by, level)]
-        bottom = [at(row) for row in range(ROWS - level, ROWS + out_by)]
-        for half, rows in enumerate((top, bottom)):
-            put = None
-            if time == STEPS:
-                def put(i, v, value, half=half):
-                    border[LOW * half + i, reg(v), :] = value
-            rows_step(time, rows, put=put)
+    for slots, low, high in FILLS:
+        for slot in slots:
+            received(slot)
+        for level in range(1, STEPS):
+            last = min(high, 2 * level)
+            if last < low:
+                continue
+            top = list(range(level - last, level - low + 1))
+            bottom = [ROWS - 1 - row for row in reversed(top)]
+            for rows, shift in ((top, 0), (bottom, 2 * LOW - ROWS)):
+                put = None
+                if level == STEPS - 1:
+                    def put(i, v, value, start=rows[0] + shift):
+                        border[start + i, reg(v), :] = value
+                rows_step(level + 1, [at(row) for row in rows], put=put)
     for direction, there in ((0, has_west), (1, has_east)):
         @pl.when(there)
         def _():
@@ -470,8 +514,8 @@
             pltpu.VMEM((4, 6, 8, 128), jnp.int32),
             pltpu.SemaphoreType.DMA((3, 3)),
             pltpu.SemaphoreType.DMA((6,)),
-            pltpu.SemaphoreType.DMA((2, 13)),
-            pltpu.SemaphoreType.DMA((2, 13)),
+            pltpu.SemaphoreType.DMA((2, SLOTS)),
+            pltpu.SemaphoreType.DMA((2, SLOTS)),
             pltpu.SemaphoreType.DMA((2, 2)),
             pltpu.SemaphoreType.DMA((2, 2)),
         ],

time: 22.6 us -> 20.6 us (0.912)
  Pallas kernels: 22.5 us -> 20.5 us
    pallas_call x1, Pallas kernels: 20.9 us -> 18.9 us  [shards(): pl.pallas_call(kernel, out_shape=(jax.ShapeDtypeStruct((ROWS, 128, 128),...]
where the time goes in v3:
time: 20.6 us; the launch traced here: 20.5 us
  Pallas kernels  20.5 us (100%)
    pallas_call x1, Pallas kernels, shards(): pl.pallas_call(kernel, out_shape=(jax.ShapeDtypeStruct((ROWS, 128, 128),...  18.9 us
    pallas_call x1, Pallas kernels, shards(): pl.pallas_call(write, out_shape=jax.ShapeDtypeStruct((4, 128, 8, 128), jn...  1.6 us

profile of v3, /device:TPU:111, one launch (start us, length us, event | category | flops | bytes accessed | tf_op | source)
XLA Modules:
  0.0 20.5 jit_solution(13849920832263155753)
XLA Ops:
  0.0 18.9 %shard_map.37 = (f32[32,128,128]{2,1,0:T(8,128)S(1)}, f32[14,128,128]{2,1,0:T(8,128)S(1)}, f32[2,32,128]{2,1,0:T(8,128)S(1)}) custom-call(f32[4,128,8,128]{3,2,1,0:T(8,128)} %bitcast.12, f32[4,128,8,128]{3,2,1,0:T(8,128)} %bitcast.13, s32[4,128,8,128]{3,2,1,0:T(8,128)} %bitcast.14), custom_call_target="tpu_custom_call" | custom-call | tf_op jit(solution)/shard_map/pallas_call | solution.py:494
  18.9 1.6 %shard_map.38 = f32[4,128,8,128]{3,2,1,0:T(8,128)} custom-call(f32[32,128,128]{2,1,0:T(8,128)S(1)} %get-tuple-element.8.ready, f32[14,128,128]{2,1,0:T(8,128)S(1)} %get-tuple-element.9.border, f32[2,32,128]{2,1,0:T(8,128)S(1)} %get-tuple-element.10.edge), custom_call_target="tpu_custom_call" | custom-call | tf_op jit(solution)/shard_map/pallas_call | solution.py:525

commit v4 on v3

--- a/solution.py
+++ b/solution.py
@@ -12,12 +12,13 @@
 ROWS = 32
 GHOST = 4
 NV = 16
+LAST = 3
 LOW, HIGH = 7, 25
 MESH = pl.DeviceIdType.MESH
 
 LINES = ((1, 2), (2, 3), (3, 4), (4, 4))
-SLOTS = 6 + len(LINES)
-FILLS = (((6, 7), 1, 4), ((8,), 5, 6), ((9,), 7, 7))
+SLOTS = 5 + len(LINES)
+FILLS = (((5, 6), 1, 4), ((7,), 5, 6), ((8,), 7, 7))
 
 
 def at(row):
@@ -77,7 +78,7 @@
     f_in, c_in, m_in,
     ready, border, edge_out,
     f_rows, c_rows, m_rows, heat, cond, east, west, south, keep,
-    edge_fc, edge_m,
+    edge_fc, edge_m, edges,
     load_sem, edge_load_sem, send_sem, recv_sem, side_send, side_recv,
 ):
     tile = lax.axis_index("tile")
@@ -105,10 +106,10 @@
         for piece, block in enumerate((0, 127)):
             for k, src in enumerate((f_in, c_in)):
                 copies.append(pltpu.make_async_copy(
-                    src.at[:, block], edge_fc.at[piece, k, pl.ds(1, 4)],
+                    src.at[:, block], edge_fc.at[piece, k],
                     edge_load_sem.at[3 * piece + k]))
             copies.append(pltpu.make_async_copy(
-                m_in.at[:, block], edge_m.at[piece, pl.ds(1, 4)],
+                m_in.at[:, block], edge_m.at[piece],
                 edge_load_sem.at[3 * piece + 2]))
         return copies
 
@@ -132,7 +133,6 @@
     for copy in edge_loads():
         copy.start()
 
-    pl.semaphore_wait(barrier, count)
 
     def rows_of(direction, near, far):
         if direction == 0:
@@ -155,15 +155,13 @@
             ref, near, far = cond, 2, 4
         elif slot == 3:
             ref, near, far = keep, 1, 3
-        elif slot < 6:
+        elif slot == 4:
             block = 1 if direction == 0 else 4
             land = 5 if direction == 0 else 0
-            if slot == 4:
-                return remote(direction, slot, edge_fc.at[:, :, block], edge_fc.at[:, :, land])
-            return remote(direction, slot, edge_m.at[:, block], edge_m.at[:, land])
+            return remote(direction, slot, edges.at[:, :, block], edges.at[:, :, land])
         else:
-            near, far = LINES[slot - 6]
-            ref = heat.at[(slot - 5) % 2]
+            near, far = LINES[slot - 5]
+            ref = heat.at[(slot - 4) % 2]
         src, dst, count = rows_of(direction, near, far)
         return remote(direction, slot, ref.at[pl.ds(at(src), count)],
                       ref.at[pl.ds(at(dst), count)])
@@ -202,10 +200,7 @@
     def side_copy(direction, kind):
         device = {"seg": seg - 1 if direction == 0 else seg + 1}
         ref = edge_m if kind else edge_fc
-        if kind:
-            src, dst = ref.at[direction, pl.ds(1, 4)], ref.at[direction + 2, pl.ds(1, 4)]
-        else:
-            src, dst = ref.at[direction, :, pl.ds(1, 4)], ref.at[direction + 2, :, pl.ds(1, 4)]
+        src, dst = ref.at[direction], ref.at[direction + 2]
         return pltpu.make_async_remote_copy(
             src_ref=src, dst_ref=dst,
             send_sem=side_send.at[direction, kind], recv_sem=side_recv.at[direction, kind],
@@ -229,6 +224,7 @@
     for row in groups[0]:
         spread_heat(row)
         spread_fixed(row)
+    pl.semaphore_wait(barrier, count)
     send(0)
     send(1)
     for copy in edge_loads():
@@ -246,8 +242,8 @@
         for j in range(3):
             spread_fixed(1 + 27 * i + j)
 
-    send(2)
-    send(3)
+    send_far(2)
+    send_far(3)
 
     zero = jnp.zeros((8, 128), jnp.float32)
     for there, first in ((has_up, -GHOST), (has_down, ROWS)):
@@ -358,25 +354,31 @@
         def _():
             side_copy(direction, 0).wait_recv()
             side_copy(direction, 1).wait_recv()
+    is_right = position()[1] < 64
+    for side, (right, left) in enumerate(((0, 3), (2, 1))):
+        for i in range(4):
+            for k in range(2):
+                edges[side, k, 1 + i] = jnp.where(
+                    is_right, edge_fc[right, k, i], edge_fc[left, k, i])
+            marks = jnp.where(is_right, edge_m[right, i], edge_m[left, i])
+            edges[side, 2, 1 + i] = jnp.where(marks != 0, 1.0, 0.0)
+    send(4)
     received(0)
     received(1)
     first_step([at(0)])
     first_step([at(ROWS - 1)])
-    send_far(6)
-    send(4)
-    send(5)
+    send_far(5)
 
     for time in range(2, STEPS + 1):
         level = time - 1
-        sweep(time, level, ROWS - level, 6)
+        sweep(time, level, ROWS - level, {2: 7, 3: 7, 6: 5}.get(level, 6))
         if time <= len(LINES):
-            send_far(5 + time)
+            send_far(4 + time)
         if time == len(LINES):
-            for slot in range(6, SLOTS):
+            for slot in (2, 3, *range(5, SLOTS)):
                 send_near(slot)
 
     received(4)
-    received(5)
     shape = (48, 128)
     lane48 = lax.broadcasted_iota(jnp.int32, shape, 1)
     row48 = lax.broadcasted_iota(jnp.int32, shape, 0)
@@ -392,23 +394,17 @@
 
     starts, all_faces = [], []
     for side in range(2):
-        right, left = ((0, 3), (2, 1))[side]
-        is_right = lane48 < 64
         first_lane = 0 if side == 0 else jnp.where(has_east, 0, 64)
         end_lane = jnp.where(has_west, 128, 64) if side == 0 else 128
         exists = ((row48 >= first_row) & (row48 < end_row)
                   & (lane48 >= first_lane) & (lane48 < end_lane))
 
         def pick(k):
-            value = jnp.where(is_right, edge_fc[right, k].reshape(shape),
-                              edge_fc[left, k].reshape(shape))
-            return jnp.where(exists, value, 0.0)
+            return jnp.where(exists, edges[side, k].reshape(shape), 0.0)
 
         f = pick(0)
         c = pick(1)
-        source = jnp.where(is_right, edge_m[right].reshape(shape),
-                           edge_m[left].reshape(shape)) != 0
-        source = jnp.logical_and(source, exists)
+        source = pick(2) > 0.5
         stay = jnp.where(jnp.logical_and(exists, jnp.logical_not(source)), 1.0, 0.0)
         faces = [stay * (FACE * (c + pltpu.roll(c, *turn))) for turn in turns]
         starts.append(jnp.where(source, 1.0, substep(f, faces)))
@@ -421,15 +417,16 @@
     for side in range(2):
         edge_out[side] = ends[side][8:40]
 
+    def in_order(first, count):
+        for row in [first + j for j in range(count)]:
+            def put(where, value, row=row):
+                ready[row, where, :] = value
+
+            finish(heat.at[STEPS % 2], at(row), edge_out, row, put)
+
     @pl.loop(0, 3)
     def _(i):
-        for j in range(6):
-            row = LOW + 6 * i + j
-
-            def put(where, value, row=row):
-                ready[row, where, :] = value
-
-            finish(heat.at[STEPS % 2], at(row), edge_out, row, put)
+        in_order(LOW + 6 * i, 6)
 
     received(2)
     received(3)
@@ -450,12 +447,15 @@
                 continue
             top = list(range(level - last, level - low + 1))
             bottom = [ROWS - 1 - row for row in reversed(top)]
-            for rows, shift in ((top, 0), (bottom, 2 * LOW - ROWS)):
+            for rows, shift in ((top, 0), (bottom, 2 * LAST - ROWS)):
                 put = None
-                if level == STEPS - 1:
+                if level == STEPS - 1 and low > 1:
                     def put(i, v, value, start=rows[0] + shift):
                         border[start + i, reg(v), :] = value
                 rows_step(level + 1, [at(row) for row in rows], put=put)
+        if low == 1:
+            in_order(LAST, LOW - LAST)
+            in_order(HIGH, LOW - LAST)
     for direction, there in ((0, has_west), (1, has_east)):
         @pl.when(there)
         def _():
@@ -467,8 +467,8 @@
     def copy(src, row, slot):
         return pltpu.make_async_copy(src, out.at[row // 8, :, row % 8], sem.at[slot])
 
-    last = [(i, i if i < LOW else HIGH + i - LOW) for i in range(2 * LOW)]
-    for row in range(LOW, HIGH):
+    last = [(i, i if i < LAST else ROWS - 2 * LAST + i) for i in range(2 * LAST)]
+    for row in range(LAST, ROWS - LAST):
         copy(ready.at[row], row, row).start()
     for i, row in last:
         def put(where, value):
@@ -476,7 +476,7 @@
 
         finish(border, i, edge, row, put)
         copy(rest.at[i], row, row).start()
-    for row in range(LOW, HIGH):
+    for row in range(LAST, ROWS - LAST):
         copy(ready.at[row], row, row).wait()
     for i, row in last:
         copy(rest.at[i], row, row).wait()
@@ -495,7 +495,7 @@
         kernel,
         out_shape=(
             jax.ShapeDtypeStruct((ROWS, 128, 128), jnp.float32),
-            jax.ShapeDtypeStruct((2 * LOW, *values), jnp.float32),
+            jax.ShapeDtypeStruct((2 * LAST, *values), jnp.float32),
             jax.ShapeDtypeStruct((2, ROWS, 128), jnp.float32),
         ),
         in_specs=[outside] * 3,
@@ -510,8 +510,9 @@
             pltpu.VMEM((wide, 8, 128), jnp.float32),
             pltpu.VMEM((wide, *values), jnp.float32),
             pltpu.VMEM((wide, *values), jnp.float32),
-            pltpu.VMEM((4, 2, 6, 8, 128), jnp.float32),
-            pltpu.VMEM((4, 6, 8, 128), jnp.int32),
+            pltpu.VMEM((4, 2, 4, 8, 128), jnp.float32),
+            pltpu.VMEM((4, 4, 8, 128), jnp.int32),
+            pltpu.VMEM((2, 3, 6, 8, 128), jnp.float32),
             pltpu.SemaphoreType.DMA((3, 3)),
             pltpu.SemaphoreType.DMA((6,)),
             pltpu.SemaphoreType.DMA((2, SLOTS)),
@@ -528,7 +529,7 @@
         in_specs=[inside] * 3,
         out_specs=outside,
         scratch_shapes=[
-            pltpu.VMEM((2 * LOW, 128, 128), jnp.float32),
+            pltpu.VMEM((2 * LAST, 128, 128), jnp.float32),
             pltpu.SemaphoreType.DMA((ROWS,)),
         ],
         compiler_params=pltpu.CompilerParams(vmem_limit_bytes=16 * 2**20),

time: 20.6 us -> 19.8 us (0.961)
  Pallas kernels: 20.5 us -> 19.7 us
    pallas_call x1, Pallas kernels: 18.9 us -> 18.1 us  [shards(): pl.pallas_call(kernel, out_shape=(jax.ShapeDtypeStruct((ROWS, 128, 128),...]
where the time goes in v4:
time: 19.8 us; the launch traced here: 19.7 us
  Pallas kernels  19.7 us (99%)
    pallas_call x1, Pallas kernels, shards(): pl.pallas_call(kernel, out_shape=(jax.ShapeDtypeStruct((ROWS, 128, 128),...  18.1 us
    pallas_call x1, Pallas kernels, shards(): pl.pallas_call(write, out_shape=jax.ShapeDtypeStruct((4, 128, 8, 128), jn...  1.59 us

profile of v4, /device:TPU:111, one launch (start us, length us, event | category | flops | bytes accessed | tf_op | source)
XLA Modules:
  0.0 19.7 jit_solution(18085615947631019645)
XLA Ops:
  0.0 18.1 %shard_map.37 = (f32[32,128,128]{2,1,0:T(8,128)S(1)}, f32[6,128,128]{2,1,0:T(8,128)S(1)}, f32[2,32,128]{2,1,0:T(8,128)S(1)}) custom-call(f32[4,128,8,128]{3,2,1,0:T(8,128)} %bitcast.12, f32[4,128,8,128]{3,2,1,0:T(8,128)} %bitcast.13, s32[4,128,8,128]{3,2,1,0:T(8,128)} %bitcast.14), custom_call_target="tpu_custom_call" | custom-call | tf_op jit(solution)/shard_map/pallas_call | solution.py:494
  18.1 1.6 %shard_map.38 = f32[4,128,8,128]{3,2,1,0:T(8,128)} custom-call(f32[32,128,128]{2,1,0:T(8,128)S(1)} %get-tuple-element.8.ready, f32[6,128,128]{2,1,0:T(8,128)S(1)} %get-tuple-element.9.border, f32[2,32,128]{2,1,0:T(8,128)S(1)} %get-tuple-element.10.edge), custom_call_target="tpu_custom_call" | custom-call | tf_op jit(solution)/shard_map/pallas_call | solution.py:526

commit v5 on v4

--- a/solution.py
+++ b/solution.py
@@ -18,7 +18,7 @@
 
 LINES = ((1, 2), (2, 3), (3, 4), (4, 4))
 SLOTS = 5 + len(LINES)
-FILLS = (((5, 6), 1, 4), ((7,), 5, 6), ((8,), 7, 7))
+FILLS = ((5, 1, 2), (6, 3, 4), (7, 5, 6), (8, 7, 7))
 
 
 def at(row):
@@ -67,11 +67,14 @@
 def finish(ref, at_row, edge, row, put):
     sub, lane = position()
     x = gather(ref, at_row)
-    for side, first, where in ((0, 0, (sub == 0) & (lane < 8)),
-                               (1, 120, (sub == 7) & (lane >= 120))):
-        patch = jnp.broadcast_to(edge[side, pl.ds(row, 1), :], (8, 128))
-        put(pl.ds(first, 8), jnp.where(where, patch, x[first:first + 8]))
-    put(pl.ds(8, 112), x[8:120])
+    for j in range(NV):
+        part = x[8 * j:8 * j + 8]
+        for side, at_end, where in ((0, 0, (sub == 0) & (lane < 8)),
+                                    (1, NV - 1, (sub == 7) & (lane >= 120))):
+            if j == at_end:
+                patch = jnp.broadcast_to(edge[side, pl.ds(row, 1), :], (8, 128))
+                part = jnp.where(where, patch, part)
+        put(j, part)
 
 
 def kernel(
@@ -225,8 +228,10 @@
         spread_heat(row)
         spread_fixed(row)
     pl.semaphore_wait(barrier, count)
-    send(0)
-    send(1)
+    send_far(0)
+    send_far(1)
+    send_near(0)
+    send_near(1)
     for copy in edge_loads():
         copy.wait()
     for direction, there in ((0, has_west), (1, has_east)):
@@ -419,8 +424,9 @@
 
     def in_order(first, count):
         for row in [first + j for j in range(count)]:
-            def put(where, value, row=row):
-                ready[row, where, :] = value
+            def put(j, value, row=row):
+                ready.reshape(4, 1024, 128)[
+                    row // 8, pl.ds(64 * j + row % 8, 8, stride=8), :] = value
 
             finish(heat.at[STEPS % 2], at(row), edge_out, row, put)
 
@@ -438,9 +444,8 @@
 
     for slot in range(SLOTS):
         sent(slot)
-    for slots, low, high in FILLS:
-        for slot in slots:
-            received(slot)
+    for slot, low, high in FILLS:
+        received(slot)
         for level in range(1, STEPS):
             last = min(high, 2 * level)
             if last < low:
@@ -449,11 +454,11 @@
             bottom = [ROWS - 1 - row for row in reversed(top)]
             for rows, shift in ((top, 0), (bottom, 2 * LAST - ROWS)):
                 put = None
-                if level == STEPS - 1 and low > 1:
+                if level == STEPS - 1 and high > LOW - LAST:
                     def put(i, v, value, start=rows[0] + shift):
                         border[start + i, reg(v), :] = value
                 rows_step(level + 1, [at(row) for row in rows], put=put)
-        if low == 1:
+        if high == LOW - LAST:
             in_order(LAST, LOW - LAST)
             in_order(HIGH, LOW - LAST)
     for direction, there in ((0, has_west), (1, has_east)):
@@ -464,22 +469,25 @@
 
 
 def write(ready, border, edge, out, rest, sem):
-    def copy(src, row, slot):
-        return pltpu.make_async_copy(src, out.at[row // 8, :, row % 8], sem.at[slot])
-
     last = [(i, i if i < LAST else ROWS - 2 * LAST + i) for i in range(2 * LAST)]
-    for row in range(LAST, ROWS - LAST):
-        copy(ready.at[row], row, row).start()
+    parts = [(0, LAST, 8 - LAST), (3, 0, 8 - LAST), (1, 0, 8), (2, 0, 8)]
+    copies = []
+    for block, first, count in parts:
+        for i in range(4):
+            piece = (block, pl.ds(32 * i, 32), pl.ds(first, count))
+            copies.append(pltpu.make_async_copy(
+                ready.at[piece], out.at[piece], sem.at[len(copies)]))
+            copies[-1].start()
     for i, row in last:
-        def put(where, value):
-            rest[i, where, :] = value
+        def put(j, value):
+            rest[i, pl.ds(8 * j, 8), :] = value
 
         finish(border, i, edge, row, put)
-        copy(rest.at[i], row, row).start()
-    for row in range(LAST, ROWS - LAST):
-        copy(ready.at[row], row, row).wait()
-    for i, row in last:
-        copy(rest.at[i], row, row).wait()
+        copies.append(pltpu.make_async_copy(
+            rest.at[i], out.at[row // 8, :, row % 8], sem.at[len(copies)]))
+        copies[-1].start()
+    for copy in copies:
+        copy.wait()
 
 
 def tiles(x):
@@ -494,7 +502,7 @@
     ready, border, edge = pl.pallas_call(
         kernel,
         out_shape=(
-            jax.ShapeDtypeStruct((ROWS, 128, 128), jnp.float32),
+            jax.ShapeDtypeStruct((4, 128, 8, 128), jnp.float32),
             jax.ShapeDtypeStruct((2 * LAST, *values), jnp.float32),
             jax.ShapeDtypeStruct((2, ROWS, 128), jnp.float32),
         ),

time: 19.8 us -> 19.9 us (level)
  no operation moved by 1% of the time
where the time goes in v5:
time: 19.9 us; the launch traced here: 19.7 us
  Pallas kernels  19.7 us (99%)
    pallas_call x1, Pallas kernels, shards(): pl.pallas_call(kernel, out_shape=(jax.ShapeDtypeStruct((4, 128, 8, 128),...  18.1 us
    pallas_call x1, Pallas kernels, shards(): pl.pallas_call(write, out_shape=jax.ShapeDtypeStruct((4, 128, 8, 128), jn...  1.6 us

profile of v5, /device:TPU:111, one launch (start us, length us, event | category | flops | bytes accessed | tf_op | source)
XLA Modules:
  0.0 19.7 jit_solution(868354866528047009)
XLA Ops:
  0.0 18.1 %shard_map.37 = (f32[4,128,8,128]{3,2,1,0:T(8,128)S(1)}, f32[6,128,128]{2,1,0:T(8,128)S(1)}, f32[2,32,128]{2,1,0:T(8,128)S(1)}) custom-call(f32[4,128,8,128]{3,2,1,0:T(8,128)} %bitcast.12, f32[4,128,8,128]{3,2,1,0:T(8,128)} %bitcast.13, s32[4,128,8,128]{3,2,1,0:T(8,128)} %bitcast.14), custom_call_target="tpu_custom_call" | custom-call | tf_op jit(solution)/shard_map/pallas_call | solution.py:502
  18.1 1.6 %shard_map.38 = f32[4,128,8,128]{3,2,1,0:T(8,128)} custom-call(f32[4,128,8,128]{3,2,1,0:T(8,128)S(1)} %get-tuple-element.8.ready, f32[6,128,128]{2,1,0:T(8,128)S(1)} %get-tuple-element.9.border, f32[2,32,128]{2,1,0:T(8,128)S(1)} %get-tuple-element.10.edge), custom_call_target="tpu_custom_call" | custom-call | tf_op jit(solution)/shard_map/pallas_call | solution.py:534
